TPU v7x, 256 devices: a whole 4x4x8 slice. The times are simulated.
256 devices in a mesh: row: 4 (over x_hi, core), col: 4 (over y), pt: 16 (over x_lo, z).
Axes of the slice: x: 4 (x_hi: 2, x_lo: 2; x = x_hi * 2 + x_lo), y: 4, z: 8, core: 2. Of those that a mesh axis runs over, the one named last changes fastest.
Arguments:
- first_factors: int32 [32, 1024, 1024], P('pt', 'row', 'col'), may hold values from 0 to 12288
- second_factors: int32 [32, 1024, 1024], P('pt', 'row', 'col'), may hold values from 0 to 12288
Outputs:
- scaled_product: float32 [45, 1024, 1024], P(None, ('row', 'pt'), 'col')
All inputs are finite; a program needn't handle non-finite values.
Results may differ from a plain program's by a relative error of at most 0.0003.
Values may be sent and summed in bfloat16 or wider, within the bound.
No kernel may reach another device: no remote copies, remote signals or barrier semaphores. Data moves between devices by JAX's collectives and lax.ppermute only.
A program may use at most 64 MiB of HBM per device.

v0:
```python
import jax
import jax.numpy as jnp
import numpy as np
from jax import lax
from jax.experimental import pallas as pl
from jax.experimental.pallas import tpu as pltpu
from jax.sharding import PartitionSpec as P

DEG = 16
POINTS = 48
COEFS = 3 * DEG - 3

modulus = 12289
inverse_modulus = 1.0 / modulus


def primitive_root():
    for candidate in range(2, modulus):
        if pow(candidate, 6144, modulus) != 1 and pow(candidate, 4096, modulus) != 1:
            return candidate
    return 0


def powers(order, row_count, column_count, inverse=False):
    root = pow(primitive_root(), (modulus - 1) // order, modulus)
    scaling = 1
    if inverse:
        root = pow(root, modulus - 2, modulus)
        scaling = pow(order, modulus - 2, modulus)
    entries = [
        [pow(root, i * j % order, modulus) * scaling % modulus for j in range(column_count)]
        for i in range(row_count)
    ]
    return np.array(entries, dtype=np.int64)


def matrix_inverse(matrix):
    size = matrix.shape[0]
    work = np.concatenate([matrix % modulus, np.eye(size, dtype=np.int64)], axis=1)
    for k in range(size):
        pivot = k + int(np.nonzero(work[k:, k])[0][0])
        work[[k, pivot]] = work[[pivot, k]]
        work[k] = work[k] * pow(int(work[k, k]), modulus - 2, modulus) % modulus
        for i in range(size):
            if i != k:
                work[i] = (work[i] - work[i, k] * work[k]) % modulus
    return work[:, size:]


def centred(values):
    values = values % modulus
    return np.where(values > modulus // 2, values - modulus, values)


def table_digits(values):
    values = centred(values)
    high = (values + 64) >> 7
    return high, values - 128 * high


def digit_table(matrix):
    of_high, of_low = table_digits(128 * matrix), table_digits(matrix)
    parts = [np.concatenate([of_high[k], of_low[k]], 1) for k in range(2)]
    return jnp.asarray(np.concatenate(parts, 0), dtype=jnp.bfloat16)


def expanded(table_ref):
    rows, columns = table_ref.shape
    wide = (columns, 8 * columns)
    place = lax.broadcasted_iota(jnp.int32, wide, 1) // 8 == lax.broadcasted_iota(jnp.int32, wide, 0)
    spread = jnp.dot(table_ref[...], place.astype(jnp.bfloat16), preferred_element_type=jnp.float32)
    full = (rows, 8, 8 * columns)
    same = lax.broadcasted_iota(jnp.int32, full, 2) % 8 == lax.broadcasted_iota(jnp.int32, full, 1)
    table = jnp.where(same, jnp.broadcast_to(spread[:, None, :], full), 0.0)
    return table.reshape(8 * rows, 8 * columns).astype(jnp.bfloat16)


def reduced(value):
    return value - jnp.floor(value * inverse_modulus + 0.5) * float(modulus)


def mixed(table, slots):
    inputs = slots.shape[0]
    half_rows = table.shape[0] // 2
    outputs = half_rows // 8
    halves = []
    for h in range(2):
        digits = jnp.concatenate(digits_of(slots[:, 8 * h : 8 * h + 8, :].reshape(inputs * 8, 256)), 0)
        sums = jnp.dot(table, digits, preferred_element_type=jnp.float32)
        top, bottom = sums[:half_rows], sums[half_rows:]
        quotient = jnp.floor(top * (128.0 * inverse_modulus) + bottom * inverse_modulus + 0.5)
        value = (top - 96.0 * quotient) * 128.0 + (bottom - quotient)
        halves.append(value.reshape(outputs, 8, 256))
    return jnp.concatenate(halves, axis=1)


def digits_of(wire):
    wire = wire.astype(jnp.int32)
    high = (wire >> 7).astype(jnp.float32).astype(jnp.bfloat16)
    low = (wire & 127).astype(jnp.float32).astype(jnp.bfloat16)
    return high, low - jnp.asarray(64.0, jnp.bfloat16)


def to_wire(value):
    return (value + 64.0).astype(jnp.int32).astype(jnp.int16)


def part_kernel(in_ref, left_ref, right_ref):
    count = left_ref.shape[1]
    left_ref[...] = in_ref[:, :count]
    right_ref[...] = in_ref[:, count:]


def spread_kernel(table_ref, in_ref, out_ref):
    count = out_ref.shape[1] // 2
    table = expanded(table_ref)
    for a in range(2):
        slots = in_ref[:, a].astype(jnp.int32).reshape(16, 16, 256)
        value = to_wire(mixed(table, slots))
        out_ref[:, a * count : (a + 1) * count] = value.reshape(16, count, 16, 256)


def middle_kernel(table_ref, in_ref, out_ref):
    slots = in_ref[...].astype(jnp.int32).reshape(-1, 16, 256)
    out_ref[...] = to_wire(mixed(expanded(table_ref), slots)).reshape(out_ref.shape)


def final_kernel(table_ref, in_ref, out_ref):
    slots = in_ref[...].astype(jnp.int32).reshape(-1, 16, 256)
    value = mixed(expanded(table_ref), slots)[:COEFS]
    value = jnp.where(value < 0.0, value + float(modulus), value)
    out_ref[...] = value / float(modulus)


def product_kernel(shift_ref, *refs):
    left_refs, right_refs, out_ref = refs[:4], refs[4:8], refs[8]
    shift = shift_ref[0]

    def store_digits(piece, scratch, place):
        high, low = digits_of(piece.reshape(256, 256))
        for part, ref in zip((high, low, high + low), scratch):
            ref[place] = part

    for j in range(out_ref.shape[1]):
        left_scratch, right_scratch = ([ref.at[j] for ref in refs[k : k + 3]] for k in (9, 12))
        for m in range(4):
            store_digits(left_refs[m][:, j], left_scratch, (slice(None), slice(256 * m, 256 * m + 256)))
            block = pl.multiple_of((m ^ shift) * 256, 256)
            store_digits(right_refs[m][:, j], right_scratch, (pl.ds(block, 256), slice(None)))
        high_high, low_low, both_both = (
            jnp.dot(left[...], right[...], preferred_element_type=jnp.float32)
            for left, right in zip(left_scratch, right_scratch)
        )
        value = reduced(high_high) * 128.0 + (both_both - high_high - low_low)
        value = reduced(reduced(value) * 128.0 + low_low)
        out_ref[:, j] = to_wire(value).reshape(16, 16, 256)


def whole(shape):
    return pl.BlockSpec(shape, lambda i: (0,) * len(shape))


def params(mebibytes=12):
    return pltpu.CompilerParams(dimension_semantics=("arbitrary",), vmem_limit_bytes=mebibytes * 1024 * 1024)


def cost(flops):
    return pl.CostEstimate(flops=flops // 8, bytes_accessed=1 << 16, transcendentals=0)


def pack(first, second):
    both = [(value + 64).astype(jnp.int16).reshape(2, 16, 16, 256) for value in (first, second)]
    return jnp.stack(both).transpose(2, 0, 1, 3, 4)


def parted(both):
    shape = both.shape[:1] + (both.shape[1] // 2,) + both.shape[2:]
    return pl.pallas_call(
        part_kernel,
        grid=(1,),
        out_shape=[jax.ShapeDtypeStruct(shape, jnp.int16)] * 2,
        in_specs=[whole(both.shape)],
        out_specs=[whole(shape)] * 2,
        compiler_params=params(4),
        cost_estimate=cost(1 << 20),
    )(both)


def spread(table, entries, pair):
    count = table.shape[0] // 32
    out_shape = (16, 2 * count, 16, 256)
    return pl.pallas_call(
        spread_kernel,
        grid=(1,),
        out_shape=jax.ShapeDtypeStruct(out_shape, jnp.int16),
        in_specs=[whole(table.shape), pl.BlockSpec((8, 2, 2, 16, 256), lambda i: (pair, 0, 0, 0, 0))],
        out_specs=whole(out_shape),
        compiler_params=params(),
        cost_estimate=cost(4 * 2 * 64 * table.shape[0] * table.shape[1] * 256),
    )(table, entries)


def middle(table, values):
    out_shape = (16, POINTS // 16, 16, 256)
    return pl.pallas_call(
        middle_kernel,
        grid=(1,),
        out_shape=jax.ShapeDtypeStruct(out_shape, jnp.int16),
        in_specs=[whole(table.shape), whole(values.shape)],
        out_specs=whole(out_shape),
        compiler_params=params(),
        cost_estimate=cost(2 * 2 * 64 * table.shape[0] * table.shape[1] * 256),
        name="middle",
    )(table, values)


def final(table, values):
    out_shape = (COEFS, 16, 256)
    return pl.pallas_call(
        final_kernel,
        grid=(1,),
        out_shape=jax.ShapeDtypeStruct(out_shape, jnp.float32),
        in_specs=[whole(table.shape), whole(values.shape)],
        out_specs=whole(out_shape),
        compiler_params=params(),
        cost_estimate=cost(2 * 2 * 64 * table.shape[0] * table.shape[1] * 256),
        name="final",
    )(table, values)


def product(shift, left, right):
    shape = left[0].shape
    return pl.pallas_call(
        product_kernel,
        grid=(1,),
        out_shape=jax.ShapeDtypeStruct(shape, jnp.int16),
        in_specs=[pl.BlockSpec(memory_space=pltpu.SMEM)] + [whole(shape)] * 8,
        out_specs=whole(shape),
        scratch_shapes=[pltpu.VMEM((shape[1], 256, 1024), jnp.bfloat16)] * 3
        + [pltpu.VMEM((shape[1], 1024, 256), jnp.bfloat16)] * 3,
        compiler_params=params(20),
        cost_estimate=cost(shape[1] * 3 * 2 * 256 * 256 * 1024),
    )(shift, *left, *right)


def exchange(value):
    return lax.all_to_all(value, "pt", split_axis=0, concat_axis=0, tiled=True)


def swapped(value, axis, bits):
    return lax.ppermute(value, axis, [(i, i ^ bits) for i in range(4)])


def along_columns(value):
    return [value] + [swapped(value, "col", m) for m in (1, 2, 3)]


def along_rows(value):
    across = swapped(value, "row", 2)
    return [value, swapped(value, "row", 1), across, swapped(across, "row", 1)]


def local(first_factors, second_factors):
    forward_two = powers(4 * DEG, POINTS, 2 * DEG)
    spread_one = digit_table(powers(2 * DEG, 2 * DEG, DEG))
    spread_two = digit_table(forward_two[:, :DEG])
    lift = forward_two[:, :DEG] @ powers(2 * DEG, 2 * DEG, 2 * DEG, True)[DEG:] % modulus
    back = matrix_inverse(powers(4 * DEG, POINTS, POINTS))
    shift = (lax.axis_index("row") ^ lax.axis_index("col")).astype(jnp.int32).reshape(1)

    entries = exchange(pack(first_factors, second_factors))
    at_one = exchange(spread(spread_one, entries, 1))
    to_two = spread(spread_two, entries, 0)
    left_one, right_one = parted(at_one)
    left_one, right_one = along_columns(left_one), along_rows(right_one)
    to_two, at_one = lax.optimization_barrier((to_two, at_one))
    at_two = exchange(to_two)
    products_one = product(shift, left_one, right_one)
    products_one, at_two = lax.optimization_barrier((products_one, at_two))
    returned = exchange(products_one)
    left_two, right_two = parted(at_two)
    left_two, right_two = along_columns(left_two), along_rows(right_two)
    to_lower = middle(digit_table(lift), returned)
    upper = along_columns(product(shift, left_two, right_two))
    lower = along_rows(exchange(to_lower))
    products_two = exchange(product(shift, upper, lower))
    return final(digit_table(back), products_two)


def solution(mesh):
    in_specs = (P("pt", "row", "col"), P("pt", "row", "col"))
    out_specs = P(None, ("row", "pt"), "col")
    return jax.shard_map(local, mesh=mesh, in_specs=in_specs, out_specs=out_specs, check_vma=False)
```

profile of v0, /device:TPU:32, one launch (start us, length us, event | category | flops | bytes accessed | tf_op | source)
XLA Modules:
  0.0 164.1 jit_solution(6623357298916493472)
XLA Ops:
  0.0 1.1 add_convert_fusion.1
  1.1 0.1 copy-done.4
  1.2 0.1 copy_bitcast_fusion
  1.3 0.0 copy-start.3
  1.3 24.3 %all_to_all.30.in_ref = s16[16,2,2,16,256]{4,3,2,1,0:T(8,128)(2,1)S(1)} all-to-all(s16[16,2,2,16,256]{4,3,2,1,0:T(8,128)(2,1)S(1)} %copy_bitcast_fusion), channel_id=1, replica_groups=mesh['row'=4,'col'=4,'pt'=16] {'pt'}, dimensions={0} | all-to-all | bytes 1048576 | tf_op jit(solution)/shard_map/all_to_all | solution.py:247
  25.6 1.6 shard_map.64
  27.2 5.4 %all-to-all-start.1 = ((s16[16,4,16,256]{3,2,1,0:T(8,128)(2,1)}), s16[16,4,16,256]{3,2,1,0:T(8,128)(2,1)S(1)}, u32[]{:S(2)}, u32[]{:S(2)}) async-start(s16[16,4,16,256]{3,2,1,0:T(8,128)(2,1)} %shard_map.64), calls=%async_computation.1 | async-start | bytes 1048576 | tf_op jit(solution)/shard_map/all_to_all | solution.py:247
  32.6 2.0 %shard_map.67 = s16[16,6,16,256]{3,2,1,0:T(8,128)(2,1)} custom-call(bf16[96,32]{1,0:T(8,128)(2,1)S(1)} %copy-done.2, s16[16,2,2,16,256]{4,3,2,1,0:T(8,128)(2,1)S(1)} %all_to_all.30.in_ref), custom_call_target="tpu_custom_call" | custom-call | flops 50331648 | bytes 65536 | tf_op jit(solution)/shard_map/pallas_call | solution.py:192
  34.6 12.7 %all-to-all-done.1.in_ref = s16[16,4,16,256]{3,2,1,0:T(8,128)(2,1)S(1)} async-done(((s16[16,4,16,256]{3,2,1,0:T(8,128)(2,1)}), s16[16,4,16,256]{3,2,1,0:T(8,128)(2,1)S(1)}, u32[]{:S(2)}, u32[]{:S(2)}) %all-to-all-start.1) | async-done | bytes 524320 | tf_op jit(solution)/shard_map/all_to_all | solution.py:247
  47.3 5.2 %all-to-all-start.2 = ((s16[16,6,16,256]{3,2,1,0:T(8,128)(2,1)}), s16[16,6,16,256]{3,2,1,0:T(8,128)(2,1)S(1)}, u32[]{:S(2)}, u32[]{:S(2)}) async-start(s16[16,6,16,256]{3,2,1,0:T(8,128)(2,1)} %shard_map.67), calls=%async_computation.2 | async-start | bytes 1572864 | tf_op jit(solution)/shard_map/all_to_all | solution.py:247
  52.5 2.8 %collective-permute-start.4 = (s16[16,2,16,256]{3,2,1,0:T(8,128)(2,1)S(1)}, s16[16,2,16,256]{3,2,1,0:T(8,128)(2,1)S(1)}, u32[]{:S(2)}, u32[]{:S(2)}) collective-permute-start(s16[16,2,16,256]{3,2,1,0:T(8,128)(2,1)S(1)} %get-tuple-element.13.refs_4_), channel_id=1, source_target_pairs={{0,128},{64,192},{128,0},{192,64},{1,129},{65,193},{129,1},{193,65... | collective-permute-start | bytes 786440 | tf_op jit(solution)/shard_map/ppermute | solution.py:251
  55.4 1.6 collective-permute-start
  56.9 2.9 %collective-permute-start.1 = (s16[16,2,16,256]{3,2,1,0:T(8,128)(2,1)S(1)}, s16[16,2,16,256]{3,2,1,0:T(8,128)(2,1)S(1)}, u32[]{:S(2)}, u32[]{:S(2)}) collective-permute-start(s16[16,2,16,256]{3,2,1,0:T(8,128)(2,1)S(1)} %get-tuple-element.12.refs_0_), channel_id=1, source_target_pairs={{0,32},{16,48},{32,0},{48,16},{1,33},{17,49},{33,1},{49,17},{2,34}... | collective-permute-start | bytes 786440 | tf_op jit(solution)/shard_map/ppermute | solution.py:251
  59.8 0.2 collective-permute-start.2
  60.1 5.3 %collective-permute-done.4.refs_6_ = s16[16,2,16,256]{3,2,1,0:T(8,128)(2,1)S(1)} collective-permute-done((s16[16,2,16,256]{3,2,1,0:T(8,128)(2,1)S(1)}, s16[16,2,16,256]{3,2,1,0:T(8,128)(2,1)S(1)}, u32[]{:S(2)}, u32[]{:S(2)}) %collective-permute-start.4) | collective-permute-done | bytes 262176 | tf_op jit(solution)/shard_map/ppermute | solution.py:251
  65.3 0.0 collective-permute-start.5
  65.3 0.0 collective-permute-done.refs_1_
  65.3 5.0 %collective-permute-done.1.refs_2_ = s16[16,2,16,256]{3,2,1,0:T(8,128)(2,1)S(1)} collective-permute-done((s16[16,2,16,256]{3,2,1,0:T(8,128)(2,1)S(1)}, s16[16,2,16,256]{3,2,1,0:T(8,128)(2,1)S(1)}, u32[]{:S(2)}, u32[]{:S(2)}) %collective-permute-start.1) | collective-permute-done | bytes 262176 | tf_op jit(solution)/shard_map/ppermute | solution.py:251
  70.3 2.6 %collective-permute-done.2.refs_3_ = s16[16,2,16,256]{3,2,1,0:T(8,128)(2,1)S(1)} collective-permute-done((s16[16,2,16,256]{3,2,1,0:T(8,128)(2,1)S(1)}, s16[16,2,16,256]{3,2,1,0:T(8,128)(2,1)S(1)}, u32[]{:S(2)}, u32[]{:S(2)}) %collective-permute-start.2) | collective-permute-done | bytes 262176 | tf_op jit(solution)/shard_map/ppermute | solution.py:251
  72.9 0.0 collective-permute-done.5.refs_7_
  72.9 2.1 %shard_map.66 = s16[16,2,16,256]{3,2,1,0:T(8,128)(2,1)S(1)} custom-call(s32[1]{0:T(128)} %bitcast.shift_ref, s16[16,2,16,256]{3,2,1,0:T(8,128)(2,1)S(1)} %get-tuple-element.12.refs_0_, s16[16,2,16,256]{3,2,1,0:T(8,128)(2,1)S(1)} %collective-permute-done.refs_1_, s16[16,2,16,256]{3,2,1,0:T(8,128)(2,1)S(1)} %collective-permute-done.1.refs_2_, ...), custom_call_target="tpu_custom_call" | custom-call | flops 100663296 | bytes 65536 | tf_op jit(solution)/shard_map/pallas_call | solution.py:233
  75.0 0.0 copy-start.1
  75.0 16.4 %all_to_all.31.in_ref = s16[16,2,16,256]{3,2,1,0:T(8,128)(2,1)S(1)} all-to-all(s16[16,2,16,256]{3,2,1,0:T(8,128)(2,1)S(1)} %shard_map.66), channel_id=1, replica_groups=mesh['row'=4,'col'=4,'pt'=16] {'pt'}, dimensions={0} | all-to-all | bytes 524288 | tf_op jit(solution)/shard_map/all_to_all | solution.py:247
  91.3 1.7 %middle.1 = s16[16,3,16,256]{3,2,1,0:T(8,128)(2,1)} custom-call(bf16[96,64]{1,0:T(8,128)(2,1)S(1)} %copy-done.1, s16[16,2,16,256]{3,2,1,0:T(8,128)(2,1)S(1)} %all_to_all.31.in_ref), custom_call_target="tpu_custom_call" | custom-call | flops 50331648 | bytes 65536 | tf_op jit(solution)/shard_map/middle/pallas_call | solution.py:205
  93.0 4.2 %all-to-all-start.4 = ((s16[16,3,16,256]{3,2,1,0:T(8,128)(2,1)}), s16[16,3,16,256]{3,2,1,0:T(8,128)(2,1)S(1)}, u32[]{:S(2)}, u32[]{:S(2)}) async-start(s16[16,3,16,256]{3,2,1,0:T(8,128)(2,1)} %middle.1), calls=%async_computation.4 | async-start | bytes 786432 | tf_op jit(solution)/shard_map/all_to_all | solution.py:247
  97.2 0.1 shard_map.68
  97.3 2.1 %collective-permute-start.10 = (s16[16,3,16,256]{3,2,1,0:T(8,128)(2,1)S(1)}, s16[16,3,16,256]{3,2,1,0:T(8,128)(2,1)S(1)}, u32[]{:S(2)}, u32[]{:S(2)}) collective-permute-start(s16[16,3,16,256]{3,2,1,0:T(8,128)(2,1)S(1)} %get-tuple-element.17.refs_4_), channel_id=1, source_target_pairs={{0,128},{64,192},{128,0},{192,64},{1,129},{65,193},{129,1},{193,65... | collective-permute-start | bytes 1179656 | tf_op jit(solution)/shard_map/ppermute | solution.py:251
  99.4 0.0 collective-permute-start.6
  99.4 2.9 %collective-permute-start.7 = (s16[16,3,16,256]{3,2,1,0:T(8,128)(2,1)S(1)}, s16[16,3,16,256]{3,2,1,0:T(8,128)(2,1)S(1)}, u32[]{:S(2)}, u32[]{:S(2)}) collective-permute-start(s16[16,3,16,256]{3,2,1,0:T(8,128)(2,1)S(1)} %get-tuple-element.16.refs_0_), channel_id=1, source_target_pairs={{0,32},{16,48},{32,0},{48,16},{1,33},{17,49},{33,1},{49,17},{2,34}... | collective-permute-start | bytes 1179656 | tf_op jit(solution)/shard_map/ppermute | solution.py:251
  102.3 1.8 %collective-permute-start.8 = (s16[16,3,16,256]{3,2,1,0:T(8,128)(2,1)S(1)}, s16[16,3,16,256]{3,2,1,0:T(8,128)(2,1)S(1)}, u32[]{:S(2)}, u32[]{:S(2)}) collective-permute-start(s16[16,3,16,256]{3,2,1,0:T(8,128)(2,1)S(1)} %get-tuple-element.16.refs_0_), channel_id=1, source_target_pairs={{0,48},{16,32},{32,16},{48,0},{1,49},{17,33},{33,17},{49,1},{2,50}... | collective-permute-start | bytes 1179656 | tf_op jit(solution)/shard_map/ppermute | solution.py:251
  104.1 0.0 collective-permute-start.9
  104.1 6.3 %collective-permute-done.10.refs_6_ = s16[16,3,16,256]{3,2,1,0:T(8,128)(2,1)S(1)} collective-permute-done((s16[16,3,16,256]{3,2,1,0:T(8,128)(2,1)S(1)}, s16[16,3,16,256]{3,2,1,0:T(8,128)(2,1)S(1)}, u32[]{:S(2)}, u32[]{:S(2)}) %collective-permute-start.10) | collective-permute-done | bytes 393248 | tf_op jit(solution)/shard_map/ppermute | solution.py:251
  110.4 1.0 collective-permute-done.6.refs_1_
  111.4 1.2 collective-permute-start.16
  112.5 5.9 %collective-permute-done.7.refs_2_ = s16[16,3,16,256]{3,2,1,0:T(8,128)(2,1)S(1)} collective-permute-done((s16[16,3,16,256]{3,2,1,0:T(8,128)(2,1)S(1)}, s16[16,3,16,256]{3,2,1,0:T(8,128)(2,1)S(1)}, u32[]{:S(2)}, u32[]{:S(2)}) %collective-permute-start.7) | collective-permute-done | bytes 393248 | tf_op jit(solution)/shard_map/ppermute | solution.py:251
  118.4 2.6 %collective-permute-done.8.refs_3_ = s16[16,3,16,256]{3,2,1,0:T(8,128)(2,1)S(1)} collective-permute-done((s16[16,3,16,256]{3,2,1,0:T(8,128)(2,1)S(1)}, s16[16,3,16,256]{3,2,1,0:T(8,128)(2,1)S(1)}, u32[]{:S(2)}, u32[]{:S(2)}) %collective-permute-start.8) | collective-permute-done | bytes 393248 | tf_op jit(solution)/shard_map/ppermute | solution.py:251
  121.0 3.1 %shard_map.69.refs_0_ = s16[16,3,16,256]{3,2,1,0:T(8,128)(2,1)S(1)} custom-call(s32[1]{0:T(128)} %bitcast.shift_ref, s16[16,3,16,256]{3,2,1,0:T(8,128)(2,1)S(1)} %get-tuple-element.16.refs_0_, s16[16,3,16,256]{3,2,1,0:T(8,128)(2,1)S(1)} %collective-permute-done.6.refs_1_, s16[16,3,16,256]{3,2,1,0:T(8,128)(2,1)S(1)} %collective-permute-done.7.refs_2_, ...), custom_call_target="tpu_custom_call" | custom-call | flops 150994944 | bytes 65536 | tf_op jit(solution)/shard_map/pallas_call | solution.py:233
  124.1 0.1 collective-permute-start.12
  124.2 1.7 %collective-permute-start.13 = (s16[16,3,16,256]{3,2,1,0:T(8,128)(2,1)S(1)}, s16[16,3,16,256]{3,2,1,0:T(8,128)(2,1)S(1)}, u32[]{:S(2)}, u32[]{:S(2)}) collective-permute-start(s16[16,3,16,256]{3,2,1,0:T(8,128)(2,1)S(1)} %shard_map.69.refs_0_), channel_id=1, source_target_pairs={{0,32},{16,48},{32,0},{48,16},{1,33},{17,49},{33,1},{49,17},{2,34}... | collective-permute-start | bytes 1179656 | tf_op jit(solution)/shard_map/ppermute | solution.py:251
  126.0 3.0 %collective-permute-start.14 = (s16[16,3,16,256]{3,2,1,0:T(8,128)(2,1)S(1)}, s16[16,3,16,256]{3,2,1,0:T(8,128)(2,1)S(1)}, u32[]{:S(2)}, u32[]{:S(2)}) collective-permute-start(s16[16,3,16,256]{3,2,1,0:T(8,128)(2,1)S(1)} %shard_map.69.refs_0_), channel_id=1, source_target_pairs={{0,48},{16,32},{32,16},{48,0},{1,49},{17,33},{33,17},{49,1},{2,50}... | collective-permute-start | bytes 1179656 | tf_op jit(solution)/shard_map/ppermute | solution.py:251
  128.9 0.5 collective-permute-start.17
  129.4 5.2 %collective-permute-done.12.refs_1_ = s16[16,3,16,256]{3,2,1,0:T(8,128)(2,1)S(1)} collective-permute-done((s16[16,3,16,256]{3,2,1,0:T(8,128)(2,1)S(1)}, s16[16,3,16,256]{3,2,1,0:T(8,128)(2,1)S(1)}, u32[]{:S(2)}, u32[]{:S(2)}) %collective-permute-start.12) | collective-permute-done | bytes 393248 | tf_op jit(solution)/shard_map/ppermute | solution.py:251
  134.6 3.5 %collective-permute-done.13.refs_2_ = s16[16,3,16,256]{3,2,1,0:T(8,128)(2,1)S(1)} collective-permute-done((s16[16,3,16,256]{3,2,1,0:T(8,128)(2,1)S(1)}, s16[16,3,16,256]{3,2,1,0:T(8,128)(2,1)S(1)}, u32[]{:S(2)}, u32[]{:S(2)}) %collective-permute-start.13) | collective-permute-done | bytes 393248 | tf_op jit(solution)/shard_map/ppermute | solution.py:251
  138.1 3.1 %collective-permute-done.14.refs_3_ = s16[16,3,16,256]{3,2,1,0:T(8,128)(2,1)S(1)} collective-permute-done((s16[16,3,16,256]{3,2,1,0:T(8,128)(2,1)S(1)}, s16[16,3,16,256]{3,2,1,0:T(8,128)(2,1)S(1)}, u32[]{:S(2)}, u32[]{:S(2)}) %collective-permute-start.14) | collective-permute-done | bytes 393248 | tf_op jit(solution)/shard_map/ppermute | solution.py:251
  141.2 3.2 %shard_map.70 = s16[16,3,16,256]{3,2,1,0:T(8,128)(2,1)S(1)} custom-call(s32[1]{0:T(128)} %bitcast.shift_ref, s16[16,3,16,256]{3,2,1,0:T(8,128)(2,1)S(1)} %shard_map.69.refs_0_, s16[16,3,16,256]{3,2,1,0:T(8,128)(2,1)S(1)} %collective-permute-done.12.refs_1_, s16[16,3,16,256]{3,2,1,0:T(8,128)(2,1)S(1)} %collective-permute-done.13.refs_2_, ...), custom_call_target="tpu_custom_call" | custom-call | flops 150994944 | bytes 65536 | tf_op jit(solution)/shard_map/pallas_call | solution.py:233
  144.3 0.0 copy-start
  144.3 17.7 %all_to_all.32.in_ref = s16[16,3,16,256]{3,2,1,0:T(8,128)(2,1)S(1)} all-to-all(s16[16,3,16,256]{3,2,1,0:T(8,128)(2,1)S(1)} %shard_map.70), channel_id=1, replica_groups=mesh['row'=4,'col'=4,'pt'=16] {'pt'}, dimensions={0} | all-to-all | bytes 786432 | tf_op jit(solution)/shard_map/all_to_all | solution.py:247
  162.0 2.0 %final.1 = f32[45,16,256]{2,1,0:T(8,128)} custom-call(bf16[96,96]{1,0:T(8,128)(2,1)S(1)} %copy-done, s16[16,3,16,256]{3,2,1,0:T(8,128)(2,1)S(1)} %all_to_all.32.in_ref), custom_call_target="tpu_custom_call" | custom-call | flops 75497472 | bytes 65536 | tf_op jit(solution)/shard_map/final/pallas_call | solution.py:219
  (19 shorter events, 0.1 us)
Async XLA Ops:
  0.0 1.2 copy-start.4
  1.3 24.3 %copy-start.3 = (bf16[64,32]{1,0:T(8,128)(2,1)S(1)}, bf16[64,32]{1,0:T(8,128)(2,1)}, u32[]{:S(2)}) copy-start(bf16[64,32]{1,0:T(8,128)(2,1)} %constant.20.clone.table_ref) | copy-start | bytes 12292
  27.2 5.4 %copy-start.2 = (bf16[96,32]{1,0:T(8,128)(2,1)S(1)}, bf16[96,32]{1,0:T(8,128)(2,1)}, u32[]{:S(2)}) copy-start(bf16[96,32]{1,0:T(8,128)(2,1)} %constant.21.clone.table_ref) | copy-start | bytes 18436
  27.2 20.1 %all-to-all-start.1 = ((s16[16,4,16,256]{3,2,1,0:T(8,128)(2,1)}), s16[16,4,16,256]{3,2,1,0:T(8,128)(2,1)S(1)}, u32[]{:S(2)}, u32[]{:S(2)}) async-start(s16[16,4,16,256]{3,2,1,0:T(8,128)(2,1)} %shard_map.64), calls=%async_computation.1 | async-start | bytes 1048576 | tf_op jit(solution)/shard_map/all_to_all | solution.py:247
  47.3 27.6 %all-to-all-start.2 = ((s16[16,6,16,256]{3,2,1,0:T(8,128)(2,1)}), s16[16,6,16,256]{3,2,1,0:T(8,128)(2,1)S(1)}, u32[]{:S(2)}, u32[]{:S(2)}) async-start(s16[16,6,16,256]{3,2,1,0:T(8,128)(2,1)} %shard_map.67), calls=%async_computation.2 | async-start | bytes 1572864 | tf_op jit(solution)/shard_map/all_to_all | solution.py:247
  52.5 12.8 %collective-permute-start.4 = (s16[16,2,16,256]{3,2,1,0:T(8,128)(2,1)S(1)}, s16[16,2,16,256]{3,2,1,0:T(8,128)(2,1)S(1)}, u32[]{:S(2)}, u32[]{:S(2)}) collective-permute-start(s16[16,2,16,256]{3,2,1,0:T(8,128)(2,1)S(1)} %get-tuple-element.13.refs_4_), channel_id=1, source_target_pairs={{0,128},{64,192},{128,0},{192,64},{1,129},{65,193},{129,1},{193,65... | collective-permute-start | bytes 786440 | tf_op jit(solution)/shard_map/ppermute | solution.py:251
  55.4 10.0 %collective-permute-start = (s16[16,2,16,256]{3,2,1,0:T(8,128)(2,1)S(1)}, s16[16,2,16,256]{3,2,1,0:T(8,128)(2,1)S(1)}, u32[]{:S(2)}, u32[]{:S(2)}) collective-permute-start(s16[16,2,16,256]{3,2,1,0:T(8,128)(2,1)S(1)} %get-tuple-element.12.refs_0_), channel_id=1, source_target_pairs={{0,16},{16,0},{32,48},{48,32},{1,17},{17,1},{33,49},{49,33},{2,18}... | collective-permute-start | bytes 786440 | tf_op jit(solution)/shard_map/ppermute | solution.py:251
  56.9 13.4 %collective-permute-start.1 = (s16[16,2,16,256]{3,2,1,0:T(8,128)(2,1)S(1)}, s16[16,2,16,256]{3,2,1,0:T(8,128)(2,1)S(1)}, u32[]{:S(2)}, u32[]{:S(2)}) collective-permute-start(s16[16,2,16,256]{3,2,1,0:T(8,128)(2,1)S(1)} %get-tuple-element.12.refs_0_), channel_id=1, source_target_pairs={{0,32},{16,48},{32,0},{48,16},{1,33},{17,49},{33,1},{49,17},{2,34}... | collective-permute-start | bytes 786440 | tf_op jit(solution)/shard_map/ppermute | solution.py:251
  59.8 13.0 %collective-permute-start.2 = (s16[16,2,16,256]{3,2,1,0:T(8,128)(2,1)S(1)}, s16[16,2,16,256]{3,2,1,0:T(8,128)(2,1)S(1)}, u32[]{:S(2)}, u32[]{:S(2)}) collective-permute-start(s16[16,2,16,256]{3,2,1,0:T(8,128)(2,1)S(1)} %get-tuple-element.12.refs_0_), channel_id=1, source_target_pairs={{0,48},{16,32},{32,16},{48,0},{1,49},{17,33},{33,17},{49,1},{2,50}... | collective-permute-start | bytes 786440 | tf_op jit(solution)/shard_map/ppermute | solution.py:251
  60.1 12.8 %collective-permute-start.3 = (s16[16,2,16,256]{3,2,1,0:T(8,128)(2,1)S(1)}, s16[16,2,16,256]{3,2,1,0:T(8,128)(2,1)S(1)}, u32[]{:S(2)}, u32[]{:S(2)}) collective-permute-start(s16[16,2,16,256]{3,2,1,0:T(8,128)(2,1)S(1)} %get-tuple-element.13.refs_4_), channel_id=1, source_target_pairs={{0,64},{64,0},{128,192},{192,128},{1,65},{65,1},{129,193},{193,129... | collective-permute-start | bytes 786440 | tf_op jit(solution)/shard_map/ppermute | solution.py:251
  65.3 7.5 %collective-permute-start.5 = (s16[16,2,16,256]{3,2,1,0:T(8,128)(2,1)S(1)}, s16[16,2,16,256]{3,2,1,0:T(8,128)(2,1)S(1)}, u32[]{:S(2)}, u32[]{:S(2)}) collective-permute-start(s16[16,2,16,256]{3,2,1,0:T(8,128)(2,1)S(1)} %collective-permute-done.4.refs_6_), channel_id=1, source_target_pairs={{0,64},{64,0},{128,192},{192,128},{1,65},{65,1},{129,193},{193,129... | collective-permute-start | bytes 786440 | tf_op jit(solution)/shard_map/ppermute | solution.py:251
  75.0 16.4 %copy-start.1 = (bf16[96,64]{1,0:T(8,128)(2,1)S(1)}, bf16[96,64]{1,0:T(8,128)(2,1)}, u32[]{:S(2)}) copy-start(bf16[96,64]{1,0:T(8,128)(2,1)} %constant.22.clone.table_ref) | copy-start | bytes 36868
  93.0 18.3 %all-to-all-start.4 = ((s16[16,3,16,256]{3,2,1,0:T(8,128)(2,1)}), s16[16,3,16,256]{3,2,1,0:T(8,128)(2,1)S(1)}, u32[]{:S(2)}, u32[]{:S(2)}) async-start(s16[16,3,16,256]{3,2,1,0:T(8,128)(2,1)} %middle.1), calls=%async_computation.4 | async-start | bytes 786432 | tf_op jit(solution)/shard_map/all_to_all | solution.py:247
  97.3 13.1 %collective-permute-start.10 = (s16[16,3,16,256]{3,2,1,0:T(8,128)(2,1)S(1)}, s16[16,3,16,256]{3,2,1,0:T(8,128)(2,1)S(1)}, u32[]{:S(2)}, u32[]{:S(2)}) collective-permute-start(s16[16,3,16,256]{3,2,1,0:T(8,128)(2,1)S(1)} %get-tuple-element.17.refs_4_), channel_id=1, source_target_pairs={{0,128},{64,192},{128,0},{192,64},{1,129},{65,193},{129,1},{193,65... | collective-permute-start | bytes 1179656 | tf_op jit(solution)/shard_map/ppermute | solution.py:251
  99.4 12.0 %collective-permute-start.6 = (s16[16,3,16,256]{3,2,1,0:T(8,128)(2,1)S(1)}, s16[16,3,16,256]{3,2,1,0:T(8,128)(2,1)S(1)}, u32[]{:S(2)}, u32[]{:S(2)}) collective-permute-start(s16[16,3,16,256]{3,2,1,0:T(8,128)(2,1)S(1)} %get-tuple-element.16.refs_0_), channel_id=1, source_target_pairs={{0,16},{16,0},{32,48},{48,32},{1,17},{17,1},{33,49},{49,33},{2,18}... | collective-permute-start | bytes 1179656 | tf_op jit(solution)/shard_map/ppermute | solution.py:251
  99.4 19.0 %collective-permute-start.7 = (s16[16,3,16,256]{3,2,1,0:T(8,128)(2,1)S(1)}, s16[16,3,16,256]{3,2,1,0:T(8,128)(2,1)S(1)}, u32[]{:S(2)}, u32[]{:S(2)}) collective-permute-start(s16[16,3,16,256]{3,2,1,0:T(8,128)(2,1)S(1)} %get-tuple-element.16.refs_0_), channel_id=1, source_target_pairs={{0,32},{16,48},{32,0},{48,16},{1,33},{17,49},{33,1},{49,17},{2,34}... | collective-permute-start | bytes 1179656 | tf_op jit(solution)/shard_map/ppermute | solution.py:251
  102.3 18.7 %collective-permute-start.8 = (s16[16,3,16,256]{3,2,1,0:T(8,128)(2,1)S(1)}, s16[16,3,16,256]{3,2,1,0:T(8,128)(2,1)S(1)}, u32[]{:S(2)}, u32[]{:S(2)}) collective-permute-start(s16[16,3,16,256]{3,2,1,0:T(8,128)(2,1)S(1)} %get-tuple-element.16.refs_0_), channel_id=1, source_target_pairs={{0,48},{16,32},{32,16},{48,0},{1,49},{17,33},{33,17},{49,1},{2,50}... | collective-permute-start | bytes 1179656 | tf_op jit(solution)/shard_map/ppermute | solution.py:251
  104.1 16.9 %collective-permute-start.9 = (s16[16,3,16,256]{3,2,1,0:T(8,128)(2,1)S(1)}, s16[16,3,16,256]{3,2,1,0:T(8,128)(2,1)S(1)}, u32[]{:S(2)}, u32[]{:S(2)}) collective-permute-start(s16[16,3,16,256]{3,2,1,0:T(8,128)(2,1)S(1)} %get-tuple-element.17.refs_4_), channel_id=1, source_target_pairs={{0,64},{64,0},{128,192},{192,128},{1,65},{65,1},{129,193},{193,129... | collective-permute-start | bytes 1179656 | tf_op jit(solution)/shard_map/ppermute | solution.py:251
  110.4 10.6 %collective-permute-start.11 = (s16[16,3,16,256]{3,2,1,0:T(8,128)(2,1)S(1)}, s16[16,3,16,256]{3,2,1,0:T(8,128)(2,1)S(1)}, u32[]{:S(2)}, u32[]{:S(2)}) collective-permute-start(s16[16,3,16,256]{3,2,1,0:T(8,128)(2,1)S(1)} %collective-permute-done.10.refs_6_), channel_id=1, source_target_pairs={{0,64},{64,0},{128,192},{192,128},{1,65},{65,1},{129,193},{193,129... | collective-permute-start | bytes 1179656 | tf_op jit(solution)/shard_map/ppermute | solution.py:251
  111.4 17.6 %collective-permute-start.16 = (s16[16,3,16,256]{3,2,1,0:T(8,128)(2,1)S(1)}, s16[16,3,16,256]{3,2,1,0:T(8,128)(2,1)S(1)}, u32[]{:S(2)}, u32[]{:S(2)}) collective-permute-start(s16[16,3,16,256]{3,2,1,0:T(8,128)(2,1)S(1)} %all-to-all-done.4.refs_4_), channel_id=1, source_target_pairs={{0,128},{64,192},{128,0},{192,64},{1,129},{65,193},{129,1},{193,65... | collective-permute-start | bytes 1179656 | tf_op jit(solution)/shard_map/ppermute | solution.py:251
  124.1 10.5 %collective-permute-start.12 = (s16[16,3,16,256]{3,2,1,0:T(8,128)(2,1)S(1)}, s16[16,3,16,256]{3,2,1,0:T(8,128)(2,1)S(1)}, u32[]{:S(2)}, u32[]{:S(2)}) collective-permute-start(s16[16,3,16,256]{3,2,1,0:T(8,128)(2,1)S(1)} %shard_map.69.refs_0_), channel_id=1, source_target_pairs={{0,16},{16,0},{32,48},{48,32},{1,17},{17,1},{33,49},{49,33},{2,18}... | collective-permute-start | bytes 1179656 | tf_op jit(solution)/shard_map/ppermute | solution.py:251
  124.2 13.8 %collective-permute-start.13 = (s16[16,3,16,256]{3,2,1,0:T(8,128)(2,1)S(1)}, s16[16,3,16,256]{3,2,1,0:T(8,128)(2,1)S(1)}, u32[]{:S(2)}, u32[]{:S(2)}) collective-permute-start(s16[16,3,16,256]{3,2,1,0:T(8,128)(2,1)S(1)} %shard_map.69.refs_0_), channel_id=1, source_target_pairs={{0,32},{16,48},{32,0},{48,16},{1,33},{17,49},{33,1},{49,17},{2,34}... | collective-permute-start | bytes 1179656 | tf_op jit(solution)/shard_map/ppermute | solution.py:251
  126.0 15.2 %collective-permute-start.14 = (s16[16,3,16,256]{3,2,1,0:T(8,128)(2,1)S(1)}, s16[16,3,16,256]{3,2,1,0:T(8,128)(2,1)S(1)}, u32[]{:S(2)}, u32[]{:S(2)}) collective-permute-start(s16[16,3,16,256]{3,2,1,0:T(8,128)(2,1)S(1)} %shard_map.69.refs_0_), channel_id=1, source_target_pairs={{0,48},{16,32},{32,16},{48,0},{1,49},{17,33},{33,17},{49,1},{2,50}... | collective-permute-start | bytes 1179656 | tf_op jit(solution)/shard_map/ppermute | solution.py:251
  128.9 12.2 %collective-permute-start.15 = (s16[16,3,16,256]{3,2,1,0:T(8,128)(2,1)S(1)}, s16[16,3,16,256]{3,2,1,0:T(8,128)(2,1)S(1)}, u32[]{:S(2)}, u32[]{:S(2)}) collective-permute-start(s16[16,3,16,256]{3,2,1,0:T(8,128)(2,1)S(1)} %all-to-all-done.4.refs_4_), channel_id=1, source_target_pairs={{0,64},{64,0},{128,192},{192,128},{1,65},{65,1},{129,193},{193,129... | collective-permute-start | bytes 1179656 | tf_op jit(solution)/shard_map/ppermute | solution.py:251
  128.9 12.2 %collective-permute-start.17 = (s16[16,3,16,256]{3,2,1,0:T(8,128)(2,1)S(1)}, s16[16,3,16,256]{3,2,1,0:T(8,128)(2,1)S(1)}, u32[]{:S(2)}, u32[]{:S(2)}) collective-permute-start(s16[16,3,16,256]{3,2,1,0:T(8,128)(2,1)S(1)} %collective-permute-done.16.refs_6_), channel_id=1, source_target_pairs={{0,64},{64,0},{128,192},{192,128},{1,65},{65,1},{129,193},{193,129... | collective-permute-start | bytes 1179656 | tf_op jit(solution)/shard_map/ppermute | solution.py:251
  144.3 17.7 %copy-start = (bf16[96,96]{1,0:T(8,128)(2,1)S(1)}, bf16[96,96]{1,0:T(8,128)(2,1)}, u32[]{:S(2)}) copy-start(bf16[96,96]{1,0:T(8,128)(2,1)} %constant.23.clone.table_ref) | copy-start | bytes 55300
where the time goes:
time: 165 us; the launch traced here: 164 us
  blocking collectives  58.3 us (35%)
  waiting for transfers between devices  53 us (32%)
  starting transfers between devices  35.5 us (22%)
  Pallas kernels  15.8 us (10%)
    all_to_all x3, blocking collectives, exchange(): return lax.all_to_all(value, 'pt', split_axis=0, concat_axis=0, tiled=True)  58.3 us
    ppermute x18, waiting for transfers between devices, swapped(): return lax.ppermute(value, axis, [(i, i ^ bits) for i in range(4)])  40.3 us
    ppermute x18, starting transfers between devices, swapped(): return lax.ppermute(value, axis, [(i, i ^ bits) for i in range(4)])  20.8 us
    all_to_all x3, starting transfers between devices, exchange(): return lax.all_to_all(value, 'pt', split_axis=0, concat_axis=0, tiled=True)  14.8 us
    all_to_all x3, waiting for transfers between devices, exchange(): return lax.all_to_all(value, 'pt', split_axis=0, concat_axis=0, tiled=True)  12.7 us
    pallas_call x3, Pallas kernels, product(): pl.pallas_call(product_kernel, grid=(1,), out_shape=jax.ShapeDtypeStruct(...  8.37 us
    pallas_call x2, Pallas kernels, spread(): pl.pallas_call(spread_kernel, grid=(1,), out_shape=jax.ShapeDtypeStruct(o...  3.59 us
  transfers between devices with their start and end apart: 21, of which 11 were waited for; matrix products, arithmetic and copies ran while one was open for 0% of the time, Pallas kernels for 4%

commit v1 on v0

--- a/solution.py
+++ b/solution.py
@@ -228,7 +228,7 @@
     )(table, values)
 
 
-def product(shift, left, right):
+def product(shift, left, right, aliases):
     shape = left[0].shape
     return pl.pallas_call(
         product_kernel,
@@ -238,6 +238,7 @@
         out_specs=whole(shape),
         scratch_shapes=[pltpu.VMEM((shape[1], 256, 1024), jnp.bfloat16)] * 3
         + [pltpu.VMEM((shape[1], 1024, 256), jnp.bfloat16)] * 3,
+        input_output_aliases=aliases,
         compiler_params=params(20),
         cost_estimate=cost(shape[1] * 3 * 2 * 256 * 256 * 1024),
     )(shift, *left, *right)
@@ -275,15 +276,15 @@
     left_one, right_one = along_columns(left_one), along_rows(right_one)
     to_two, at_one = lax.optimization_barrier((to_two, at_one))
     at_two = exchange(to_two)
-    products_one = product(shift, left_one, right_one)
+    products_one = product(shift, left_one, right_one, {})
     products_one, at_two = lax.optimization_barrier((products_one, at_two))
     returned = exchange(products_one)
     left_two, right_two = parted(at_two)
     left_two, right_two = along_columns(left_two), along_rows(right_two)
     to_lower = middle(digit_table(lift), returned)
-    upper = along_columns(product(shift, left_two, right_two))
+    upper = along_columns(product(shift, left_two, right_two, {1: 0}))
     lower = along_rows(exchange(to_lower))
-    products_two = exchange(product(shift, upper, lower))
+    products_two = exchange(product(shift, upper, lower, {1: 0}))
     return final(digit_table(back), products_two)
 
 

time: 165 us -> 165 us (level)
  no operation moved by 1% of the time
where the time goes in v1:
time: 165 us; the launch traced here: 164 us
  blocking collectives  58.4 us (35%)
  waiting for transfers between devices  53 us (32%)
  starting transfers between devices  35.5 us (22%)
  Pallas kernels  15.8 us (10%)
    all_to_all x3, blocking collectives, exchange(): return lax.all_to_all(value, 'pt', split_axis=0, concat_axis=0, tiled=True)  58.4 us
    ppermute x18, waiting for transfers between devices, swapped(): return lax.ppermute(value, axis, [(i, i ^ bits) for i in range(4)])  40.3 us
    ppermute x18, starting transfers between devices, swapped(): return lax.ppermute(value, axis, [(i, i ^ bits) for i in range(4)])  20.8 us
    all_to_all x3, starting transfers between devices, exchange(): return lax.all_to_all(value, 'pt', split_axis=0, concat_axis=0, tiled=True)  14.8 us
    all_to_all x3, waiting for transfers between devices, exchange(): return lax.all_to_all(value, 'pt', split_axis=0, concat_axis=0, tiled=True)  12.7 us
    pallas_call x3, Pallas kernels, product(): pl.pallas_call(product_kernel, grid=(1,), out_shape=jax.ShapeDtypeStruct(...  8.37 us
    pallas_call x2, Pallas kernels, spread(): pl.pallas_call(spread_kernel, grid=(1,), out_shape=jax.ShapeDtypeStruct(o...  3.59 us
  transfers between devices with their start and end apart: 21, of which 11 were waited for; matrix products, arithmetic and copies ran while one was open for 0% of the time, Pallas kernels for 4%

profile of v1, /device:TPU:32, one launch (start us, length us, event | category | flops | bytes accessed | tf_op | source)
XLA Modules:
  0.0 164.1 jit_solution(14750724079562265464)
XLA Ops:
  0.0 1.1 add_convert_fusion.1
  1.1 0.1 copy-done.4
  1.2 0.1 copy_bitcast_fusion
  1.3 0.0 copy-start.3
  1.3 24.3 %all_to_all.30.in_ref = s16[16,2,2,16,256]{4,3,2,1,0:T(8,128)(2,1)S(1)} all-to-all(s16[16,2,2,16,256]{4,3,2,1,0:T(8,128)(2,1)S(1)} %copy_bitcast_fusion), channel_id=1, replica_groups=mesh['row'=4,'col'=4,'pt'=16] {'pt'}, dimensions={0} | all-to-all | bytes 1048576 | tf_op jit(solution)/shard_map/all_to_all | solution.py:248
  25.6 1.6 shard_map.64
  27.2 5.4 %all-to-all-start.1 = ((s16[16,4,16,256]{3,2,1,0:T(8,128)(2,1)}), s16[16,4,16,256]{3,2,1,0:T(8,128)(2,1)S(1)}, u32[]{:S(2)}, u32[]{:S(2)}) async-start(s16[16,4,16,256]{3,2,1,0:T(8,128)(2,1)} %shard_map.64), calls=%async_computation.1 | async-start | bytes 1048576 | tf_op jit(solution)/shard_map/all_to_all | solution.py:248
  32.6 2.0 %shard_map.67 = s16[16,6,16,256]{3,2,1,0:T(8,128)(2,1)} custom-call(bf16[96,32]{1,0:T(8,128)(2,1)S(1)} %copy-done.2, s16[16,2,2,16,256]{4,3,2,1,0:T(8,128)(2,1)S(1)} %all_to_all.30.in_ref), custom_call_target="tpu_custom_call" | custom-call | flops 50331648 | bytes 65536 | tf_op jit(solution)/shard_map/pallas_call | solution.py:192
  34.6 12.7 %all-to-all-done.1.in_ref = s16[16,4,16,256]{3,2,1,0:T(8,128)(2,1)S(1)} async-done(((s16[16,4,16,256]{3,2,1,0:T(8,128)(2,1)}), s16[16,4,16,256]{3,2,1,0:T(8,128)(2,1)S(1)}, u32[]{:S(2)}, u32[]{:S(2)}) %all-to-all-start.1) | async-done | bytes 524320 | tf_op jit(solution)/shard_map/all_to_all | solution.py:248
  47.3 5.2 %all-to-all-start.2 = ((s16[16,6,16,256]{3,2,1,0:T(8,128)(2,1)}), s16[16,6,16,256]{3,2,1,0:T(8,128)(2,1)S(1)}, u32[]{:S(2)}, u32[]{:S(2)}) async-start(s16[16,6,16,256]{3,2,1,0:T(8,128)(2,1)} %shard_map.67), calls=%async_computation.2 | async-start | bytes 1572864 | tf_op jit(solution)/shard_map/all_to_all | solution.py:248
  52.5 2.8 %collective-permute-start.4 = (s16[16,2,16,256]{3,2,1,0:T(8,128)(2,1)S(1)}, s16[16,2,16,256]{3,2,1,0:T(8,128)(2,1)S(1)}, u32[]{:S(2)}, u32[]{:S(2)}) collective-permute-start(s16[16,2,16,256]{3,2,1,0:T(8,128)(2,1)S(1)} %get-tuple-element.13.refs_4_), channel_id=1, source_target_pairs={{0,128},{64,192},{128,0},{192,64},{1,129},{65,193},{129,1},{193,65... | collective-permute-start | bytes 786440 | tf_op jit(solution)/shard_map/ppermute | solution.py:252
  55.4 1.6 collective-permute-start
  56.9 2.9 %collective-permute-start.1 = (s16[16,2,16,256]{3,2,1,0:T(8,128)(2,1)S(1)}, s16[16,2,16,256]{3,2,1,0:T(8,128)(2,1)S(1)}, u32[]{:S(2)}, u32[]{:S(2)}) collective-permute-start(s16[16,2,16,256]{3,2,1,0:T(8,128)(2,1)S(1)} %get-tuple-element.12.refs_0_), channel_id=1, source_target_pairs={{0,32},{16,48},{32,0},{48,16},{1,33},{17,49},{33,1},{49,17},{2,34}... | collective-permute-start | bytes 786440 | tf_op jit(solution)/shard_map/ppermute | solution.py:252
  59.8 0.2 collective-permute-start.2
  60.1 5.3 %collective-permute-done.4.refs_6_ = s16[16,2,16,256]{3,2,1,0:T(8,128)(2,1)S(1)} collective-permute-done((s16[16,2,16,256]{3,2,1,0:T(8,128)(2,1)S(1)}, s16[16,2,16,256]{3,2,1,0:T(8,128)(2,1)S(1)}, u32[]{:S(2)}, u32[]{:S(2)}) %collective-permute-start.4) | collective-permute-done | bytes 262176 | tf_op jit(solution)/shard_map/ppermute | solution.py:252
  65.3 0.0 collective-permute-start.5
  65.3 0.0 collective-permute-done.refs_1_
  65.3 5.0 %collective-permute-done.1.refs_2_ = s16[16,2,16,256]{3,2,1,0:T(8,128)(2,1)S(1)} collective-permute-done((s16[16,2,16,256]{3,2,1,0:T(8,128)(2,1)S(1)}, s16[16,2,16,256]{3,2,1,0:T(8,128)(2,1)S(1)}, u32[]{:S(2)}, u32[]{:S(2)}) %collective-permute-start.1) | collective-permute-done | bytes 262176 | tf_op jit(solution)/shard_map/ppermute | solution.py:252
  70.3 2.6 %collective-permute-done.2.refs_3_ = s16[16,2,16,256]{3,2,1,0:T(8,128)(2,1)S(1)} collective-permute-done((s16[16,2,16,256]{3,2,1,0:T(8,128)(2,1)S(1)}, s16[16,2,16,256]{3,2,1,0:T(8,128)(2,1)S(1)}, u32[]{:S(2)}, u32[]{:S(2)}) %collective-permute-start.2) | collective-permute-done | bytes 262176 | tf_op jit(solution)/shard_map/ppermute | solution.py:252
  72.9 0.0 collective-permute-done.5.refs_7_
  72.9 2.1 %shard_map.66 = s16[16,2,16,256]{3,2,1,0:T(8,128)(2,1)S(1)} custom-call(s32[1]{0:T(128)} %bitcast.shift_ref, s16[16,2,16,256]{3,2,1,0:T(8,128)(2,1)S(1)} %get-tuple-element.12.refs_0_, s16[16,2,16,256]{3,2,1,0:T(8,128)(2,1)S(1)} %collective-permute-done.refs_1_, s16[16,2,16,256]{3,2,1,0:T(8,128)(2,1)S(1)} %collective-permute-done.1.refs_2_, ...), custom_call_target="tpu_custom_call" | custom-call | flops 100663296 | bytes 65536 | tf_op jit(solution)/shard_map/pallas_call | solution.py:233
  75.0 0.0 copy-start.1
  75.0 16.4 %all_to_all.31.in_ref = s16[16,2,16,256]{3,2,1,0:T(8,128)(2,1)S(1)} all-to-all(s16[16,2,16,256]{3,2,1,0:T(8,128)(2,1)S(1)} %shard_map.66), channel_id=1, replica_groups=mesh['row'=4,'col'=4,'pt'=16] {'pt'}, dimensions={0} | all-to-all | bytes 524288 | tf_op jit(solution)/shard_map/all_to_all | solution.py:248
  91.3 1.7 %middle.1 = s16[16,3,16,256]{3,2,1,0:T(8,128)(2,1)} custom-call(bf16[96,64]{1,0:T(8,128)(2,1)S(1)} %copy-done.1, s16[16,2,16,256]{3,2,1,0:T(8,128)(2,1)S(1)} %all_to_all.31.in_ref), custom_call_target="tpu_custom_call" | custom-call | flops 50331648 | bytes 65536 | tf_op jit(solution)/shard_map/middle/pallas_call | solution.py:205
  93.0 4.2 %all-to-all-start.4 = ((s16[16,3,16,256]{3,2,1,0:T(8,128)(2,1)}), s16[16,3,16,256]{3,2,1,0:T(8,128)(2,1)S(1)}, u32[]{:S(2)}, u32[]{:S(2)}) async-start(s16[16,3,16,256]{3,2,1,0:T(8,128)(2,1)} %middle.1), calls=%async_computation.4 | async-start | bytes 786432 | tf_op jit(solution)/shard_map/all_to_all | solution.py:248
  97.2 0.1 shard_map.68
  97.3 2.1 %collective-permute-start.10 = (s16[16,3,16,256]{3,2,1,0:T(8,128)(2,1)S(1)}, s16[16,3,16,256]{3,2,1,0:T(8,128)(2,1)S(1)}, u32[]{:S(2)}, u32[]{:S(2)}) collective-permute-start(s16[16,3,16,256]{3,2,1,0:T(8,128)(2,1)S(1)} %get-tuple-element.17.refs_4_), channel_id=1, source_target_pairs={{0,128},{64,192},{128,0},{192,64},{1,129},{65,193},{129,1},{193,65... | collective-permute-start | bytes 1179656 | tf_op jit(solution)/shard_map/ppermute | solution.py:252
  99.4 0.0 collective-permute-start.6
  99.4 2.9 %collective-permute-start.7 = (s16[16,3,16,256]{3,2,1,0:T(8,128)(2,1)S(1)}, s16[16,3,16,256]{3,2,1,0:T(8,128)(2,1)S(1)}, u32[]{:S(2)}, u32[]{:S(2)}) collective-permute-start(s16[16,3,16,256]{3,2,1,0:T(8,128)(2,1)S(1)} %get-tuple-element.16.refs_0_), channel_id=1, source_target_pairs={{0,32},{16,48},{32,0},{48,16},{1,33},{17,49},{33,1},{49,17},{2,34}... | collective-permute-start | bytes 1179656 | tf_op jit(solution)/shard_map/ppermute | solution.py:252
  102.3 1.8 %collective-permute-start.8 = (s16[16,3,16,256]{3,2,1,0:T(8,128)(2,1)S(1)}, s16[16,3,16,256]{3,2,1,0:T(8,128)(2,1)S(1)}, u32[]{:S(2)}, u32[]{:S(2)}) collective-permute-start(s16[16,3,16,256]{3,2,1,0:T(8,128)(2,1)S(1)} %get-tuple-element.16.refs_0_), channel_id=1, source_target_pairs={{0,48},{16,32},{32,16},{48,0},{1,49},{17,33},{33,17},{49,1},{2,50}... | collective-permute-start | bytes 1179656 | tf_op jit(solution)/shard_map/ppermute | solution.py:252
  104.1 0.0 collective-permute-start.9
  104.1 6.3 %collective-permute-done.10.refs_6_ = s16[16,3,16,256]{3,2,1,0:T(8,128)(2,1)S(1)} collective-permute-done((s16[16,3,16,256]{3,2,1,0:T(8,128)(2,1)S(1)}, s16[16,3,16,256]{3,2,1,0:T(8,128)(2,1)S(1)}, u32[]{:S(2)}, u32[]{:S(2)}) %collective-permute-start.10) | collective-permute-done | bytes 393248 | tf_op jit(solution)/shard_map/ppermute | solution.py:252
  110.4 1.0 collective-permute-done.6.refs_1_
  111.4 1.2 collective-permute-start.16
  112.5 5.9 %collective-permute-done.7.refs_2_ = s16[16,3,16,256]{3,2,1,0:T(8,128)(2,1)S(1)} collective-permute-done((s16[16,3,16,256]{3,2,1,0:T(8,128)(2,1)S(1)}, s16[16,3,16,256]{3,2,1,0:T(8,128)(2,1)S(1)}, u32[]{:S(2)}, u32[]{:S(2)}) %collective-permute-start.7) | collective-permute-done | bytes 393248 | tf_op jit(solution)/shard_map/ppermute | solution.py:252
  118.4 2.6 %collective-permute-done.8.refs_3_ = s16[16,3,16,256]{3,2,1,0:T(8,128)(2,1)S(1)} collective-permute-done((s16[16,3,16,256]{3,2,1,0:T(8,128)(2,1)S(1)}, s16[16,3,16,256]{3,2,1,0:T(8,128)(2,1)S(1)}, u32[]{:S(2)}, u32[]{:S(2)}) %collective-permute-start.8) | collective-permute-done | bytes 393248 | tf_op jit(solution)/shard_map/ppermute | solution.py:252
  121.0 3.1 %shard_map.69.refs_0_ = s16[16,3,16,256]{3,2,1,0:T(8,128)(2,1)S(1)} custom-call(s32[1]{0:T(128)} %bitcast.shift_ref, s16[16,3,16,256]{3,2,1,0:T(8,128)(2,1)S(1)} %get-tuple-element.16.refs_0_, s16[16,3,16,256]{3,2,1,0:T(8,128)(2,1)S(1)} %collective-permute-done.6.refs_1_, ...), custom_call_target="tpu_custom_call", output_to_operand_aliasing={{}: (1, {})} | custom-call | flops 150994944 | bytes 65536 | tf_op jit(solution)/shard_map/pallas_call | solution.py:233
  124.1 0.1 collective-permute-start.12
  124.2 1.7 %collective-permute-start.13 = (s16[16,3,16,256]{3,2,1,0:T(8,128)(2,1)S(1)}, s16[16,3,16,256]{3,2,1,0:T(8,128)(2,1)S(1)}, u32[]{:S(2)}, u32[]{:S(2)}) collective-permute-start(s16[16,3,16,256]{3,2,1,0:T(8,128)(2,1)S(1)} %shard_map.69.refs_0_), channel_id=1, source_target_pairs={{0,32},{16,48},{32,0},{48,16},{1,33},{17,49},{33,1},{49,17},{2,34}... | collective-permute-start | bytes 1179656 | tf_op jit(solution)/shard_map/ppermute | solution.py:252
  126.0 3.0 %collective-permute-start.14 = (s16[16,3,16,256]{3,2,1,0:T(8,128)(2,1)S(1)}, s16[16,3,16,256]{3,2,1,0:T(8,128)(2,1)S(1)}, u32[]{:S(2)}, u32[]{:S(2)}) collective-permute-start(s16[16,3,16,256]{3,2,1,0:T(8,128)(2,1)S(1)} %shard_map.69.refs_0_), channel_id=1, source_target_pairs={{0,48},{16,32},{32,16},{48,0},{1,49},{17,33},{33,17},{49,1},{2,50}... | collective-permute-start | bytes 1179656 | tf_op jit(solution)/shard_map/ppermute | solution.py:252
  128.9 0.5 collective-permute-start.17
  129.4 5.1 %collective-permute-done.12.refs_1_ = s16[16,3,16,256]{3,2,1,0:T(8,128)(2,1)S(1)} collective-permute-done((s16[16,3,16,256]{3,2,1,0:T(8,128)(2,1)S(1)}, s16[16,3,16,256]{3,2,1,0:T(8,128)(2,1)S(1)}, u32[]{:S(2)}, u32[]{:S(2)}) %collective-permute-start.12) | collective-permute-done | bytes 393248 | tf_op jit(solution)/shard_map/ppermute | solution.py:252
  134.6 3.5 %collective-permute-done.13.refs_2_ = s16[16,3,16,256]{3,2,1,0:T(8,128)(2,1)S(1)} collective-permute-done((s16[16,3,16,256]{3,2,1,0:T(8,128)(2,1)S(1)}, s16[16,3,16,256]{3,2,1,0:T(8,128)(2,1)S(1)}, u32[]{:S(2)}, u32[]{:S(2)}) %collective-permute-start.13) | collective-permute-done | bytes 393248 | tf_op jit(solution)/shard_map/ppermute | solution.py:252
  138.1 3.1 %collective-permute-done.14.refs_3_ = s16[16,3,16,256]{3,2,1,0:T(8,128)(2,1)S(1)} collective-permute-done((s16[16,3,16,256]{3,2,1,0:T(8,128)(2,1)S(1)}, s16[16,3,16,256]{3,2,1,0:T(8,128)(2,1)S(1)}, u32[]{:S(2)}, u32[]{:S(2)}) %collective-permute-start.14) | collective-permute-done | bytes 393248 | tf_op jit(solution)/shard_map/ppermute | solution.py:252
  141.2 3.1 %shard_map.70 = s16[16,3,16,256]{3,2,1,0:T(8,128)(2,1)S(1)} custom-call(s32[1]{0:T(128)} %bitcast.shift_ref, s16[16,3,16,256]{3,2,1,0:T(8,128)(2,1)S(1)} %shard_map.69.refs_0_, s16[16,3,16,256]{3,2,1,0:T(8,128)(2,1)S(1)} %collective-permute-done.12.refs_1_, ...), custom_call_target="tpu_custom_call", output_to_operand_aliasing={{}: (1, {})} | custom-call | flops 150994944 | bytes 65536 | tf_op jit(solution)/shard_map/pallas_call | solution.py:233
  144.3 0.0 copy-start
  144.3 17.7 %all_to_all.32.in_ref = s16[16,3,16,256]{3,2,1,0:T(8,128)(2,1)S(1)} all-to-all(s16[16,3,16,256]{3,2,1,0:T(8,128)(2,1)S(1)} %shard_map.70), channel_id=1, replica_groups=mesh['row'=4,'col'=4,'pt'=16] {'pt'}, dimensions={0} | all-to-all | bytes 786432 | tf_op jit(solution)/shard_map/all_to_all | solution.py:248
  162.0 2.0 %final.1 = f32[45,16,256]{2,1,0:T(8,128)} custom-call(bf16[96,96]{1,0:T(8,128)(2,1)S(1)} %copy-done, s16[16,3,16,256]{3,2,1,0:T(8,128)(2,1)S(1)} %all_to_all.32.in_ref), custom_call_target="tpu_custom_call" | custom-call | flops 75497472 | bytes 65536 | tf_op jit(solution)/shard_map/final/pallas_call | solution.py:219
  (19 shorter events, 0.1 us)
Async XLA Ops:
  0.0 1.2 copy-start.4
  1.3 24.3 %copy-start.3 = (bf16[64,32]{1,0:T(8,128)(2,1)S(1)}, bf16[64,32]{1,0:T(8,128)(2,1)}, u32[]{:S(2)}) copy-start(bf16[64,32]{1,0:T(8,128)(2,1)} %constant.20.clone.table_ref) | copy-start | bytes 12292
  27.2 5.4 %copy-start.2 = (bf16[96,32]{1,0:T(8,128)(2,1)S(1)}, bf16[96,32]{1,0:T(8,128)(2,1)}, u32[]{:S(2)}) copy-start(bf16[96,32]{1,0:T(8,128)(2,1)} %constant.21.clone.table_ref) | copy-start | bytes 18436
  27.2 20.1 %all-to-all-start.1 = ((s16[16,4,16,256]{3,2,1,0:T(8,128)(2,1)}), s16[16,4,16,256]{3,2,1,0:T(8,128)(2,1)S(1)}, u32[]{:S(2)}, u32[]{:S(2)}) async-start(s16[16,4,16,256]{3,2,1,0:T(8,128)(2,1)} %shard_map.64), calls=%async_computation.1 | async-start | bytes 1048576 | tf_op jit(solution)/shard_map/all_to_all | solution.py:248
  47.3 27.6 %all-to-all-start.2 = ((s16[16,6,16,256]{3,2,1,0:T(8,128)(2,1)}), s16[16,6,16,256]{3,2,1,0:T(8,128)(2,1)S(1)}, u32[]{:S(2)}, u32[]{:S(2)}) async-start(s16[16,6,16,256]{3,2,1,0:T(8,128)(2,1)} %shard_map.67), calls=%async_computation.2 | async-start | bytes 1572864 | tf_op jit(solution)/shard_map/all_to_all | solution.py:248
  52.5 12.8 %collective-permute-start.4 = (s16[16,2,16,256]{3,2,1,0:T(8,128)(2,1)S(1)}, s16[16,2,16,256]{3,2,1,0:T(8,128)(2,1)S(1)}, u32[]{:S(2)}, u32[]{:S(2)}) collective-permute-start(s16[16,2,16,256]{3,2,1,0:T(8,128)(2,1)S(1)} %get-tuple-element.13.refs_4_), channel_id=1, source_target_pairs={{0,128},{64,192},{128,0},{192,64},{1,129},{65,193},{129,1},{193,65... | collective-permute-start | bytes 786440 | tf_op jit(solution)/shard_map/ppermute | solution.py:252
  55.4 10.0 %collective-permute-start = (s16[16,2,16,256]{3,2,1,0:T(8,128)(2,1)S(1)}, s16[16,2,16,256]{3,2,1,0:T(8,128)(2,1)S(1)}, u32[]{:S(2)}, u32[]{:S(2)}) collective-permute-start(s16[16,2,16,256]{3,2,1,0:T(8,128)(2,1)S(1)} %get-tuple-element.12.refs_0_), channel_id=1, source_target_pairs={{0,16},{16,0},{32,48},{48,32},{1,17},{17,1},{33,49},{49,33},{2,18}... | collective-permute-start | bytes 786440 | tf_op jit(solution)/shard_map/ppermute | solution.py:252
  56.9 13.4 %collective-permute-start.1 = (s16[16,2,16,256]{3,2,1,0:T(8,128)(2,1)S(1)}, s16[16,2,16,256]{3,2,1,0:T(8,128)(2,1)S(1)}, u32[]{:S(2)}, u32[]{:S(2)}) collective-permute-start(s16[16,2,16,256]{3,2,1,0:T(8,128)(2,1)S(1)} %get-tuple-element.12.refs_0_), channel_id=1, source_target_pairs={{0,32},{16,48},{32,0},{48,16},{1,33},{17,49},{33,1},{49,17},{2,34}... | collective-permute-start | bytes 786440 | tf_op jit(solution)/shard_map/ppermute | solution.py:252
  59.8 13.0 %collective-permute-start.2 = (s16[16,2,16,256]{3,2,1,0:T(8,128)(2,1)S(1)}, s16[16,2,16,256]{3,2,1,0:T(8,128)(2,1)S(1)}, u32[]{:S(2)}, u32[]{:S(2)}) collective-permute-start(s16[16,2,16,256]{3,2,1,0:T(8,128)(2,1)S(1)} %get-tuple-element.12.refs_0_), channel_id=1, source_target_pairs={{0,48},{16,32},{32,16},{48,0},{1,49},{17,33},{33,17},{49,1},{2,50}... | collective-permute-start | bytes 786440 | tf_op jit(solution)/shard_map/ppermute | solution.py:252
  60.1 12.8 %collective-permute-start.3 = (s16[16,2,16,256]{3,2,1,0:T(8,128)(2,1)S(1)}, s16[16,2,16,256]{3,2,1,0:T(8,128)(2,1)S(1)}, u32[]{:S(2)}, u32[]{:S(2)}) collective-permute-start(s16[16,2,16,256]{3,2,1,0:T(8,128)(2,1)S(1)} %get-tuple-element.13.refs_4_), channel_id=1, source_target_pairs={{0,64},{64,0},{128,192},{192,128},{1,65},{65,1},{129,193},{193,129... | collective-permute-start | bytes 786440 | tf_op jit(solution)/shard_map/ppermute | solution.py:252
  65.3 7.5 %collective-permute-start.5 = (s16[16,2,16,256]{3,2,1,0:T(8,128)(2,1)S(1)}, s16[16,2,16,256]{3,2,1,0:T(8,128)(2,1)S(1)}, u32[]{:S(2)}, u32[]{:S(2)}) collective-permute-start(s16[16,2,16,256]{3,2,1,0:T(8,128)(2,1)S(1)} %collective-permute-done.4.refs_6_), channel_id=1, source_target_pairs={{0,64},{64,0},{128,192},{192,128},{1,65},{65,1},{129,193},{193,129... | collective-permute-start | bytes 786440 | tf_op jit(solution)/shard_map/ppermute | solution.py:252
  75.0 16.4 %copy-start.1 = (bf16[96,64]{1,0:T(8,128)(2,1)S(1)}, bf16[96,64]{1,0:T(8,128)(2,1)}, u32[]{:S(2)}) copy-start(bf16[96,64]{1,0:T(8,128)(2,1)} %constant.22.clone.table_ref) | copy-start | bytes 36868
  93.0 18.3 %all-to-all-start.4 = ((s16[16,3,16,256]{3,2,1,0:T(8,128)(2,1)}), s16[16,3,16,256]{3,2,1,0:T(8,128)(2,1)S(1)}, u32[]{:S(2)}, u32[]{:S(2)}) async-start(s16[16,3,16,256]{3,2,1,0:T(8,128)(2,1)} %middle.1), calls=%async_computation.4 | async-start | bytes 786432 | tf_op jit(solution)/shard_map/all_to_all | solution.py:248
  97.3 13.1 %collective-permute-start.10 = (s16[16,3,16,256]{3,2,1,0:T(8,128)(2,1)S(1)}, s16[16,3,16,256]{3,2,1,0:T(8,128)(2,1)S(1)}, u32[]{:S(2)}, u32[]{:S(2)}) collective-permute-start(s16[16,3,16,256]{3,2,1,0:T(8,128)(2,1)S(1)} %get-tuple-element.17.refs_4_), channel_id=1, source_target_pairs={{0,128},{64,192},{128,0},{192,64},{1,129},{65,193},{129,1},{193,65... | collective-permute-start | bytes 1179656 | tf_op jit(solution)/shard_map/ppermute | solution.py:252
  99.4 12.0 %collective-permute-start.6 = (s16[16,3,16,256]{3,2,1,0:T(8,128)(2,1)S(1)}, s16[16,3,16,256]{3,2,1,0:T(8,128)(2,1)S(1)}, u32[]{:S(2)}, u32[]{:S(2)}) collective-permute-start(s16[16,3,16,256]{3,2,1,0:T(8,128)(2,1)S(1)} %get-tuple-element.16.refs_0_), channel_id=1, source_target_pairs={{0,16},{16,0},{32,48},{48,32},{1,17},{17,1},{33,49},{49,33},{2,18}... | collective-permute-start | bytes 1179656 | tf_op jit(solution)/shard_map/ppermute | solution.py:252
  99.4 19.0 %collective-permute-start.7 = (s16[16,3,16,256]{3,2,1,0:T(8,128)(2,1)S(1)}, s16[16,3,16,256]{3,2,1,0:T(8,128)(2,1)S(1)}, u32[]{:S(2)}, u32[]{:S(2)}) collective-permute-start(s16[16,3,16,256]{3,2,1,0:T(8,128)(2,1)S(1)} %get-tuple-element.16.refs_0_), channel_id=1, source_target_pairs={{0,32},{16,48},{32,0},{48,16},{1,33},{17,49},{33,1},{49,17},{2,34}... | collective-permute-start | bytes 1179656 | tf_op jit(solution)/shard_map/ppermute | solution.py:252
  102.3 18.7 %collective-permute-start.8 = (s16[16,3,16,256]{3,2,1,0:T(8,128)(2,1)S(1)}, s16[16,3,16,256]{3,2,1,0:T(8,128)(2,1)S(1)}, u32[]{:S(2)}, u32[]{:S(2)}) collective-permute-start(s16[16,3,16,256]{3,2,1,0:T(8,128)(2,1)S(1)} %get-tuple-element.16.refs_0_), channel_id=1, source_target_pairs={{0,48},{16,32},{32,16},{48,0},{1,49},{17,33},{33,17},{49,1},{2,50}... | collective-permute-start | bytes 1179656 | tf_op jit(solution)/shard_map/ppermute | solution.py:252
  104.1 16.9 %collective-permute-start.9 = (s16[16,3,16,256]{3,2,1,0:T(8,128)(2,1)S(1)}, s16[16,3,16,256]{3,2,1,0:T(8,128)(2,1)S(1)}, u32[]{:S(2)}, u32[]{:S(2)}) collective-permute-start(s16[16,3,16,256]{3,2,1,0:T(8,128)(2,1)S(1)} %get-tuple-element.17.refs_4_), channel_id=1, source_target_pairs={{0,64},{64,0},{128,192},{192,128},{1,65},{65,1},{129,193},{193,129... | collective-permute-start | bytes 1179656 | tf_op jit(solution)/shard_map/ppermute | solution.py:252
  110.4 10.6 %collective-permute-start.11 = (s16[16,3,16,256]{3,2,1,0:T(8,128)(2,1)S(1)}, s16[16,3,16,256]{3,2,1,0:T(8,128)(2,1)S(1)}, u32[]{:S(2)}, u32[]{:S(2)}) collective-permute-start(s16[16,3,16,256]{3,2,1,0:T(8,128)(2,1)S(1)} %collective-permute-done.10.refs_6_), channel_id=1, source_target_pairs={{0,64},{64,0},{128,192},{192,128},{1,65},{65,1},{129,193},{193,129... | collective-permute-start | bytes 1179656 | tf_op jit(solution)/shard_map/ppermute | solution.py:252
  111.4 17.6 %collective-permute-start.16 = (s16[16,3,16,256]{3,2,1,0:T(8,128)(2,1)S(1)}, s16[16,3,16,256]{3,2,1,0:T(8,128)(2,1)S(1)}, u32[]{:S(2)}, u32[]{:S(2)}) collective-permute-start(s16[16,3,16,256]{3,2,1,0:T(8,128)(2,1)S(1)} %all-to-all-done.4.refs_4_), channel_id=1, source_target_pairs={{0,128},{64,192},{128,0},{192,64},{1,129},{65,193},{129,1},{193,65... | collective-permute-start | bytes 1179656 | tf_op jit(solution)/shard_map/ppermute | solution.py:252
  124.1 10.4 %collective-permute-start.12 = (s16[16,3,16,256]{3,2,1,0:T(8,128)(2,1)S(1)}, s16[16,3,16,256]{3,2,1,0:T(8,128)(2,1)S(1)}, u32[]{:S(2)}, u32[]{:S(2)}) collective-permute-start(s16[16,3,16,256]{3,2,1,0:T(8,128)(2,1)S(1)} %shard_map.69.refs_0_), channel_id=1, source_target_pairs={{0,16},{16,0},{32,48},{48,32},{1,17},{17,1},{33,49},{49,33},{2,18}... | collective-permute-start | bytes 1179656 | tf_op jit(solution)/shard_map/ppermute | solution.py:252
  124.2 13.8 %collective-permute-start.13 = (s16[16,3,16,256]{3,2,1,0:T(8,128)(2,1)S(1)}, s16[16,3,16,256]{3,2,1,0:T(8,128)(2,1)S(1)}, u32[]{:S(2)}, u32[]{:S(2)}) collective-permute-start(s16[16,3,16,256]{3,2,1,0:T(8,128)(2,1)S(1)} %shard_map.69.refs_0_), channel_id=1, source_target_pairs={{0,32},{16,48},{32,0},{48,16},{1,33},{17,49},{33,1},{49,17},{2,34}... | collective-permute-start | bytes 1179656 | tf_op jit(solution)/shard_map/ppermute | solution.py:252
  126.0 15.2 %collective-permute-start.14 = (s16[16,3,16,256]{3,2,1,0:T(8,128)(2,1)S(1)}, s16[16,3,16,256]{3,2,1,0:T(8,128)(2,1)S(1)}, u32[]{:S(2)}, u32[]{:S(2)}) collective-permute-start(s16[16,3,16,256]{3,2,1,0:T(8,128)(2,1)S(1)} %shard_map.69.refs_0_), channel_id=1, source_target_pairs={{0,48},{16,32},{32,16},{48,0},{1,49},{17,33},{33,17},{49,1},{2,50}... | collective-permute-start | bytes 1179656 | tf_op jit(solution)/shard_map/ppermute | solution.py:252
  128.9 12.2 %collective-permute-start.15 = (s16[16,3,16,256]{3,2,1,0:T(8,128)(2,1)S(1)}, s16[16,3,16,256]{3,2,1,0:T(8,128)(2,1)S(1)}, u32[]{:S(2)}, u32[]{:S(2)}) collective-permute-start(s16[16,3,16,256]{3,2,1,0:T(8,128)(2,1)S(1)} %all-to-all-done.4.refs_4_), channel_id=1, source_target_pairs={{0,64},{64,0},{128,192},{192,128},{1,65},{65,1},{129,193},{193,129... | collective-permute-start | bytes 1179656 | tf_op jit(solution)/shard_map/ppermute | solution.py:252
  128.9 12.2 %collective-permute-start.17 = (s16[16,3,16,256]{3,2,1,0:T(8,128)(2,1)S(1)}, s16[16,3,16,256]{3,2,1,0:T(8,128)(2,1)S(1)}, u32[]{:S(2)}, u32[]{:S(2)}) collective-permute-start(s16[16,3,16,256]{3,2,1,0:T(8,128)(2,1)S(1)} %collective-permute-done.16.refs_6_), channel_id=1, source_target_pairs={{0,64},{64,0},{128,192},{192,128},{1,65},{65,1},{129,193},{193,129... | collective-permute-start | bytes 1179656 | tf_op jit(solution)/shard_map/ppermute | solution.py:252
  144.3 17.7 %copy-start = (bf16[96,96]{1,0:T(8,128)(2,1)S(1)}, bf16[96,96]{1,0:T(8,128)(2,1)}, u32[]{:S(2)}) copy-start(bf16[96,96]{1,0:T(8,128)(2,1)} %constant.23.clone.table_ref) | copy-start | bytes 55300

commit v2 on v1

--- a/solution.py
+++ b/solution.py
@@ -138,21 +138,21 @@
 
     def store_digits(piece, scratch, place):
         high, low = digits_of(piece.reshape(256, 256))
-        for part, ref in zip((high, low, high + low), scratch):
+        for part, ref in zip((high, low), scratch):
             ref[place] = part
 
     for j in range(out_ref.shape[1]):
-        left_scratch, right_scratch = ([ref.at[j] for ref in refs[k : k + 3]] for k in (9, 12))
+        left_scratch, right_scratch = ([ref.at[j] for ref in refs[k : k + 2]] for k in (9, 11))
         for m in range(4):
             store_digits(left_refs[m][:, j], left_scratch, (slice(None), slice(256 * m, 256 * m + 256)))
             block = pl.multiple_of((m ^ shift) * 256, 256)
             store_digits(right_refs[m][:, j], right_scratch, (pl.ds(block, 256), slice(None)))
-        high_high, low_low, both_both = (
-            jnp.dot(left[...], right[...], preferred_element_type=jnp.float32)
-            for left, right in zip(left_scratch, right_scratch)
-        )
-        value = reduced(high_high) * 128.0 + (both_both - high_high - low_low)
-        value = reduced(reduced(value) * 128.0 + low_low)
+        sums = [
+            [jnp.dot(left[...], right[...], preferred_element_type=jnp.float32) for right in right_scratch]
+            for left in left_scratch
+        ]
+        value = reduced(sums[0][0]) * 128.0 + (sums[0][1] + sums[1][0])
+        value = reduced(reduced(value) * 128.0 + sums[1][1])
         out_ref[:, j] = to_wire(value).reshape(16, 16, 256)
 
 
@@ -236,8 +236,8 @@
         out_shape=jax.ShapeDtypeStruct(shape, jnp.int16),
         in_specs=[pl.BlockSpec(memory_space=pltpu.SMEM)] + [whole(shape)] * 8,
         out_specs=whole(shape),
-        scratch_shapes=[pltpu.VMEM((shape[1], 256, 1024), jnp.bfloat16)] * 3
-        + [pltpu.VMEM((shape[1], 1024, 256), jnp.bfloat16)] * 3,
+        scratch_shapes=[pltpu.VMEM((shape[1], 256, 1024), jnp.bfloat16)] * 2
+        + [pltpu.VMEM((shape[1], 1024, 256), jnp.bfloat16)] * 2,
         input_output_aliases=aliases,
         compiler_params=params(20),
         cost_estimate=cost(shape[1] * 3 * 2 * 256 * 256 * 1024),

time: 165 us -> 164 us (level)
  no operation moved by 1% of the time
where the time goes in v2:
time: 164 us; the launch traced here: 163 us
  blocking collectives  58.3 us (36%)
  waiting for transfers between devices  53 us (32%)
  starting transfers between devices  35.5 us (22%)
  Pallas kernels  15.2 us (9%)
    all_to_all x3, blocking collectives, exchange(): return lax.all_to_all(value, 'pt', split_axis=0, concat_axis=0, tiled=True)  58.3 us
    ppermute x18, waiting for transfers between devices, swapped(): return lax.ppermute(value, axis, [(i, i ^ bits) for i in range(4)])  40.3 us
    ppermute x18, starting transfers between devices, swapped(): return lax.ppermute(value, axis, [(i, i ^ bits) for i in range(4)])  20.8 us
    all_to_all x3, starting transfers between devices, exchange(): return lax.all_to_all(value, 'pt', split_axis=0, concat_axis=0, tiled=True)  14.8 us
    all_to_all x3, waiting for transfers between devices, exchange(): return lax.all_to_all(value, 'pt', split_axis=0, concat_axis=0, tiled=True)  12.7 us
    pallas_call x3, Pallas kernels, product(): pl.pallas_call(product_kernel, grid=(1,), out_shape=jax.ShapeDtypeStruct(...  7.77 us
    pallas_call x2, Pallas kernels, spread(): pl.pallas_call(spread_kernel, grid=(1,), out_shape=jax.ShapeDtypeStruct(o...  3.59 us
  transfers between devices with their start and end apart: 21, of which 11 were waited for; matrix products, arithmetic and copies ran while one was open for 0% of the time, Pallas kernels for 4%

profile of v2, /device:TPU:32, one launch (start us, length us, event | category | flops | bytes accessed | tf_op | source)
XLA Modules:
  0.0 163.4 jit_solution(13821282724149324049)
XLA Ops:
  0.0 1.1 add_convert_fusion.1
  1.1 0.1 copy-done.4
  1.2 0.1 copy_bitcast_fusion
  1.3 0.0 copy-start.3
  1.3 24.3 %all_to_all.30.in_ref = s16[16,2,2,16,256]{4,3,2,1,0:T(8,128)(2,1)S(1)} all-to-all(s16[16,2,2,16,256]{4,3,2,1,0:T(8,128)(2,1)S(1)} %copy_bitcast_fusion), channel_id=1, replica_groups=mesh['row'=4,'col'=4,'pt'=16] {'pt'}, dimensions={0} | all-to-all | bytes 1048576 | tf_op jit(solution)/shard_map/all_to_all | solution.py:248
  25.6 1.6 shard_map.64
  27.2 5.4 %all-to-all-start.1 = ((s16[16,4,16,256]{3,2,1,0:T(8,128)(2,1)}), s16[16,4,16,256]{3,2,1,0:T(8,128)(2,1)S(1)}, u32[]{:S(2)}, u32[]{:S(2)}) async-start(s16[16,4,16,256]{3,2,1,0:T(8,128)(2,1)} %shard_map.64), calls=%async_computation.1 | async-start | bytes 1048576 | tf_op jit(solution)/shard_map/all_to_all | solution.py:248
  32.6 2.0 %shard_map.67 = s16[16,6,16,256]{3,2,1,0:T(8,128)(2,1)} custom-call(bf16[96,32]{1,0:T(8,128)(2,1)S(1)} %copy-done.2, s16[16,2,2,16,256]{4,3,2,1,0:T(8,128)(2,1)S(1)} %all_to_all.30.in_ref), custom_call_target="tpu_custom_call" | custom-call | flops 50331648 | bytes 65536 | tf_op jit(solution)/shard_map/pallas_call | solution.py:192
  34.6 12.7 %all-to-all-done.1.in_ref = s16[16,4,16,256]{3,2,1,0:T(8,128)(2,1)S(1)} async-done(((s16[16,4,16,256]{3,2,1,0:T(8,128)(2,1)}), s16[16,4,16,256]{3,2,1,0:T(8,128)(2,1)S(1)}, u32[]{:S(2)}, u32[]{:S(2)}) %all-to-all-start.1) | async-done | bytes 524320 | tf_op jit(solution)/shard_map/all_to_all | solution.py:248
  47.3 5.2 %all-to-all-start.2 = ((s16[16,6,16,256]{3,2,1,0:T(8,128)(2,1)}), s16[16,6,16,256]{3,2,1,0:T(8,128)(2,1)S(1)}, u32[]{:S(2)}, u32[]{:S(2)}) async-start(s16[16,6,16,256]{3,2,1,0:T(8,128)(2,1)} %shard_map.67), calls=%async_computation.2 | async-start | bytes 1572864 | tf_op jit(solution)/shard_map/all_to_all | solution.py:248
  52.5 2.8 %collective-permute-start.4 = (s16[16,2,16,256]{3,2,1,0:T(8,128)(2,1)S(1)}, s16[16,2,16,256]{3,2,1,0:T(8,128)(2,1)S(1)}, u32[]{:S(2)}, u32[]{:S(2)}) collective-permute-start(s16[16,2,16,256]{3,2,1,0:T(8,128)(2,1)S(1)} %get-tuple-element.13.refs_4_), channel_id=1, source_target_pairs={{0,128},{64,192},{128,0},{192,64},{1,129},{65,193},{129,1},{193,65... | collective-permute-start | bytes 786440 | tf_op jit(solution)/shard_map/ppermute | solution.py:252
  55.4 1.6 collective-permute-start
  56.9 2.9 %collective-permute-start.1 = (s16[16,2,16,256]{3,2,1,0:T(8,128)(2,1)S(1)}, s16[16,2,16,256]{3,2,1,0:T(8,128)(2,1)S(1)}, u32[]{:S(2)}, u32[]{:S(2)}) collective-permute-start(s16[16,2,16,256]{3,2,1,0:T(8,128)(2,1)S(1)} %get-tuple-element.12.refs_0_), channel_id=1, source_target_pairs={{0,32},{16,48},{32,0},{48,16},{1,33},{17,49},{33,1},{49,17},{2,34}... | collective-permute-start | bytes 786440 | tf_op jit(solution)/shard_map/ppermute | solution.py:252
  59.8 0.2 collective-permute-start.2
  60.1 5.3 %collective-permute-done.4.refs_6_ = s16[16,2,16,256]{3,2,1,0:T(8,128)(2,1)S(1)} collective-permute-done((s16[16,2,16,256]{3,2,1,0:T(8,128)(2,1)S(1)}, s16[16,2,16,256]{3,2,1,0:T(8,128)(2,1)S(1)}, u32[]{:S(2)}, u32[]{:S(2)}) %collective-permute-start.4) | collective-permute-done | bytes 262176 | tf_op jit(solution)/shard_map/ppermute | solution.py:252
  65.3 0.0 collective-permute-start.5
  65.3 0.0 collective-permute-done.refs_1_
  65.3 5.0 %collective-permute-done.1.refs_2_ = s16[16,2,16,256]{3,2,1,0:T(8,128)(2,1)S(1)} collective-permute-done((s16[16,2,16,256]{3,2,1,0:T(8,128)(2,1)S(1)}, s16[16,2,16,256]{3,2,1,0:T(8,128)(2,1)S(1)}, u32[]{:S(2)}, u32[]{:S(2)}) %collective-permute-start.1) | collective-permute-done | bytes 262176 | tf_op jit(solution)/shard_map/ppermute | solution.py:252
  70.3 2.6 %collective-permute-done.2.refs_3_ = s16[16,2,16,256]{3,2,1,0:T(8,128)(2,1)S(1)} collective-permute-done((s16[16,2,16,256]{3,2,1,0:T(8,128)(2,1)S(1)}, s16[16,2,16,256]{3,2,1,0:T(8,128)(2,1)S(1)}, u32[]{:S(2)}, u32[]{:S(2)}) %collective-permute-start.2) | collective-permute-done | bytes 262176 | tf_op jit(solution)/shard_map/ppermute | solution.py:252
  72.9 0.0 collective-permute-done.5.refs_7_
  72.9 2.0 %shard_map.66 = s16[16,2,16,256]{3,2,1,0:T(8,128)(2,1)S(1)} custom-call(s32[1]{0:T(128)} %bitcast.shift_ref, s16[16,2,16,256]{3,2,1,0:T(8,128)(2,1)S(1)} %get-tuple-element.12.refs_0_, s16[16,2,16,256]{3,2,1,0:T(8,128)(2,1)S(1)} %collective-permute-done.refs_1_, s16[16,2,16,256]{3,2,1,0:T(8,128)(2,1)S(1)} %collective-permute-done.1.refs_2_, ...), custom_call_target="tpu_custom_call" | custom-call | flops 100663296 | bytes 65536 | tf_op jit(solution)/shard_map/pallas_call | solution.py:233
  74.9 0.0 copy-start.1
  74.9 16.4 %all_to_all.31.in_ref = s16[16,2,16,256]{3,2,1,0:T(8,128)(2,1)S(1)} all-to-all(s16[16,2,16,256]{3,2,1,0:T(8,128)(2,1)S(1)} %shard_map.66), channel_id=1, replica_groups=mesh['row'=4,'col'=4,'pt'=16] {'pt'}, dimensions={0} | all-to-all | bytes 524288 | tf_op jit(solution)/shard_map/all_to_all | solution.py:248
  91.3 1.7 %middle.1 = s16[16,3,16,256]{3,2,1,0:T(8,128)(2,1)} custom-call(bf16[96,64]{1,0:T(8,128)(2,1)S(1)} %copy-done.1, s16[16,2,16,256]{3,2,1,0:T(8,128)(2,1)S(1)} %all_to_all.31.in_ref), custom_call_target="tpu_custom_call" | custom-call | flops 50331648 | bytes 65536 | tf_op jit(solution)/shard_map/middle/pallas_call | solution.py:205
  92.9 4.2 %all-to-all-start.4 = ((s16[16,3,16,256]{3,2,1,0:T(8,128)(2,1)}), s16[16,3,16,256]{3,2,1,0:T(8,128)(2,1)S(1)}, u32[]{:S(2)}, u32[]{:S(2)}) async-start(s16[16,3,16,256]{3,2,1,0:T(8,128)(2,1)} %middle.1), calls=%async_computation.4 | async-start | bytes 786432 | tf_op jit(solution)/shard_map/all_to_all | solution.py:248
  97.1 0.1 shard_map.68
  97.2 2.1 %collective-permute-start.10 = (s16[16,3,16,256]{3,2,1,0:T(8,128)(2,1)S(1)}, s16[16,3,16,256]{3,2,1,0:T(8,128)(2,1)S(1)}, u32[]{:S(2)}, u32[]{:S(2)}) collective-permute-start(s16[16,3,16,256]{3,2,1,0:T(8,128)(2,1)S(1)} %get-tuple-element.17.refs_4_), channel_id=1, source_target_pairs={{0,128},{64,192},{128,0},{192,64},{1,129},{65,193},{129,1},{193,65... | collective-permute-start | bytes 1179656 | tf_op jit(solution)/shard_map/ppermute | solution.py:252
  99.3 0.0 collective-permute-start.6
  99.3 2.9 %collective-permute-start.7 = (s16[16,3,16,256]{3,2,1,0:T(8,128)(2,1)S(1)}, s16[16,3,16,256]{3,2,1,0:T(8,128)(2,1)S(1)}, u32[]{:S(2)}, u32[]{:S(2)}) collective-permute-start(s16[16,3,16,256]{3,2,1,0:T(8,128)(2,1)S(1)} %get-tuple-element.16.refs_0_), channel_id=1, source_target_pairs={{0,32},{16,48},{32,0},{48,16},{1,33},{17,49},{33,1},{49,17},{2,34}... | collective-permute-start | bytes 1179656 | tf_op jit(solution)/shard_map/ppermute | solution.py:252
  102.2 1.8 %collective-permute-start.8 = (s16[16,3,16,256]{3,2,1,0:T(8,128)(2,1)S(1)}, s16[16,3,16,256]{3,2,1,0:T(8,128)(2,1)S(1)}, u32[]{:S(2)}, u32[]{:S(2)}) collective-permute-start(s16[16,3,16,256]{3,2,1,0:T(8,128)(2,1)S(1)} %get-tuple-element.16.refs_0_), channel_id=1, source_target_pairs={{0,48},{16,32},{32,16},{48,0},{1,49},{17,33},{33,17},{49,1},{2,50}... | collective-permute-start | bytes 1179656 | tf_op jit(solution)/shard_map/ppermute | solution.py:252
  104.0 6.3 %collective-permute-done.10.refs_6_ = s16[16,3,16,256]{3,2,1,0:T(8,128)(2,1)S(1)} collective-permute-done((s16[16,3,16,256]{3,2,1,0:T(8,128)(2,1)S(1)}, s16[16,3,16,256]{3,2,1,0:T(8,128)(2,1)S(1)}, u32[]{:S(2)}, u32[]{:S(2)}) %collective-permute-start.10) | collective-permute-done | bytes 393248 | tf_op jit(solution)/shard_map/ppermute | solution.py:252
  110.3 0.0 collective-permute-start.11
  110.3 1.0 collective-permute-done.6.refs_1_
  111.3 1.1 collective-permute-start.16
  112.4 5.9 %collective-permute-done.7.refs_2_ = s16[16,3,16,256]{3,2,1,0:T(8,128)(2,1)S(1)} collective-permute-done((s16[16,3,16,256]{3,2,1,0:T(8,128)(2,1)S(1)}, s16[16,3,16,256]{3,2,1,0:T(8,128)(2,1)S(1)}, u32[]{:S(2)}, u32[]{:S(2)}) %collective-permute-start.7) | collective-permute-done | bytes 393248 | tf_op jit(solution)/shard_map/ppermute | solution.py:252
  118.3 2.6 %collective-permute-done.8.refs_3_ = s16[16,3,16,256]{3,2,1,0:T(8,128)(2,1)S(1)} collective-permute-done((s16[16,3,16,256]{3,2,1,0:T(8,128)(2,1)S(1)}, s16[16,3,16,256]{3,2,1,0:T(8,128)(2,1)S(1)}, u32[]{:S(2)}, u32[]{:S(2)}) %collective-permute-start.8) | collective-permute-done | bytes 393248 | tf_op jit(solution)/shard_map/ppermute | solution.py:252
  120.9 2.9 %shard_map.69.refs_0_ = s16[16,3,16,256]{3,2,1,0:T(8,128)(2,1)S(1)} custom-call(s32[1]{0:T(128)} %bitcast.shift_ref, s16[16,3,16,256]{3,2,1,0:T(8,128)(2,1)S(1)} %get-tuple-element.16.refs_0_, s16[16,3,16,256]{3,2,1,0:T(8,128)(2,1)S(1)} %collective-permute-done.6.refs_1_, ...), custom_call_target="tpu_custom_call", output_to_operand_aliasing={{}: (1, {})} | custom-call | flops 150994944 | bytes 65536 | tf_op jit(solution)/shard_map/pallas_call | solution.py:233
  123.8 0.1 collective-permute-start.12
  123.9 1.7 %collective-permute-start.13 = (s16[16,3,16,256]{3,2,1,0:T(8,128)(2,1)S(1)}, s16[16,3,16,256]{3,2,1,0:T(8,128)(2,1)S(1)}, u32[]{:S(2)}, u32[]{:S(2)}) collective-permute-start(s16[16,3,16,256]{3,2,1,0:T(8,128)(2,1)S(1)} %shard_map.69.refs_0_), channel_id=1, source_target_pairs={{0,32},{16,48},{32,0},{48,16},{1,33},{17,49},{33,1},{49,17},{2,34}... | collective-permute-start | bytes 1179656 | tf_op jit(solution)/shard_map/ppermute | solution.py:252
  125.6 2.9 %collective-permute-start.14 = (s16[16,3,16,256]{3,2,1,0:T(8,128)(2,1)S(1)}, s16[16,3,16,256]{3,2,1,0:T(8,128)(2,1)S(1)}, u32[]{:S(2)}, u32[]{:S(2)}) collective-permute-start(s16[16,3,16,256]{3,2,1,0:T(8,128)(2,1)S(1)} %shard_map.69.refs_0_), channel_id=1, source_target_pairs={{0,48},{16,32},{32,16},{48,0},{1,49},{17,33},{33,17},{49,1},{2,50}... | collective-permute-start | bytes 1179656 | tf_op jit(solution)/shard_map/ppermute | solution.py:252
  128.6 0.5 collective-permute-start.17
  129.1 5.2 %collective-permute-done.12.refs_1_ = s16[16,3,16,256]{3,2,1,0:T(8,128)(2,1)S(1)} collective-permute-done((s16[16,3,16,256]{3,2,1,0:T(8,128)(2,1)S(1)}, s16[16,3,16,256]{3,2,1,0:T(8,128)(2,1)S(1)}, u32[]{:S(2)}, u32[]{:S(2)}) %collective-permute-start.12) | collective-permute-done | bytes 393248 | tf_op jit(solution)/shard_map/ppermute | solution.py:252
  134.2 3.5 %collective-permute-done.13.refs_2_ = s16[16,3,16,256]{3,2,1,0:T(8,128)(2,1)S(1)} collective-permute-done((s16[16,3,16,256]{3,2,1,0:T(8,128)(2,1)S(1)}, s16[16,3,16,256]{3,2,1,0:T(8,128)(2,1)S(1)}, u32[]{:S(2)}, u32[]{:S(2)}) %collective-permute-start.13) | collective-permute-done | bytes 393248 | tf_op jit(solution)/shard_map/ppermute | solution.py:252
  137.8 3.0 %collective-permute-done.14.refs_3_ = s16[16,3,16,256]{3,2,1,0:T(8,128)(2,1)S(1)} collective-permute-done((s16[16,3,16,256]{3,2,1,0:T(8,128)(2,1)S(1)}, s16[16,3,16,256]{3,2,1,0:T(8,128)(2,1)S(1)}, u32[]{:S(2)}, u32[]{:S(2)}) %collective-permute-start.14) | collective-permute-done | bytes 393248 | tf_op jit(solution)/shard_map/ppermute | solution.py:252
  140.8 2.9 %shard_map.70 = s16[16,3,16,256]{3,2,1,0:T(8,128)(2,1)S(1)} custom-call(s32[1]{0:T(128)} %bitcast.shift_ref, s16[16,3,16,256]{3,2,1,0:T(8,128)(2,1)S(1)} %shard_map.69.refs_0_, s16[16,3,16,256]{3,2,1,0:T(8,128)(2,1)S(1)} %collective-permute-done.12.refs_1_, ...), custom_call_target="tpu_custom_call", output_to_operand_aliasing={{}: (1, {})} | custom-call | flops 150994944 | bytes 65536 | tf_op jit(solution)/shard_map/pallas_call | solution.py:233
  143.7 0.0 copy-start
  143.7 17.7 %all_to_all.32.in_ref = s16[16,3,16,256]{3,2,1,0:T(8,128)(2,1)S(1)} all-to-all(s16[16,3,16,256]{3,2,1,0:T(8,128)(2,1)S(1)} %shard_map.70), channel_id=1, replica_groups=mesh['row'=4,'col'=4,'pt'=16] {'pt'}, dimensions={0} | all-to-all | bytes 786432 | tf_op jit(solution)/shard_map/all_to_all | solution.py:248
  161.4 2.0 %final.1 = f32[45,16,256]{2,1,0:T(8,128)} custom-call(bf16[96,96]{1,0:T(8,128)(2,1)S(1)} %copy-done, s16[16,3,16,256]{3,2,1,0:T(8,128)(2,1)S(1)} %all_to_all.32.in_ref), custom_call_target="tpu_custom_call" | custom-call | flops 75497472 | bytes 65536 | tf_op jit(solution)/shard_map/final/pallas_call | solution.py:219
  (19 shorter events, 0.1 us)
Async XLA Ops:
  0.0 1.2 copy-start.4
  1.3 24.3 %copy-start.3 = (bf16[64,32]{1,0:T(8,128)(2,1)S(1)}, bf16[64,32]{1,0:T(8,128)(2,1)}, u32[]{:S(2)}) copy-start(bf16[64,32]{1,0:T(8,128)(2,1)} %constant.20.clone.table_ref) | copy-start | bytes 12292
  27.2 5.4 %copy-start.2 = (bf16[96,32]{1,0:T(8,128)(2,1)S(1)}, bf16[96,32]{1,0:T(8,128)(2,1)}, u32[]{:S(2)}) copy-start(bf16[96,32]{1,0:T(8,128)(2,1)} %constant.21.clone.table_ref) | copy-start | bytes 18436
  27.2 20.1 %all-to-all-start.1 = ((s16[16,4,16,256]{3,2,1,0:T(8,128)(2,1)}), s16[16,4,16,256]{3,2,1,0:T(8,128)(2,1)S(1)}, u32[]{:S(2)}, u32[]{:S(2)}) async-start(s16[16,4,16,256]{3,2,1,0:T(8,128)(2,1)} %shard_map.64), calls=%async_computation.1 | async-start | bytes 1048576 | tf_op jit(solution)/shard_map/all_to_all | solution.py:248
  47.3 27.5 %all-to-all-start.2 = ((s16[16,6,16,256]{3,2,1,0:T(8,128)(2,1)}), s16[16,6,16,256]{3,2,1,0:T(8,128)(2,1)S(1)}, u32[]{:S(2)}, u32[]{:S(2)}) async-start(s16[16,6,16,256]{3,2,1,0:T(8,128)(2,1)} %shard_map.67), calls=%async_computation.2 | async-start | bytes 1572864 | tf_op jit(solution)/shard_map/all_to_all | solution.py:248
  52.5 12.8 %collective-permute-start.4 = (s16[16,2,16,256]{3,2,1,0:T(8,128)(2,1)S(1)}, s16[16,2,16,256]{3,2,1,0:T(8,128)(2,1)S(1)}, u32[]{:S(2)}, u32[]{:S(2)}) collective-permute-start(s16[16,2,16,256]{3,2,1,0:T(8,128)(2,1)S(1)} %get-tuple-element.13.refs_4_), channel_id=1, source_target_pairs={{0,128},{64,192},{128,0},{192,64},{1,129},{65,193},{129,1},{193,65... | collective-permute-start | bytes 786440 | tf_op jit(solution)/shard_map/ppermute | solution.py:252
  55.4 10.0 %collective-permute-start = (s16[16,2,16,256]{3,2,1,0:T(8,128)(2,1)S(1)}, s16[16,2,16,256]{3,2,1,0:T(8,128)(2,1)S(1)}, u32[]{:S(2)}, u32[]{:S(2)}) collective-permute-start(s16[16,2,16,256]{3,2,1,0:T(8,128)(2,1)S(1)} %get-tuple-element.12.refs_0_), channel_id=1, source_target_pairs={{0,16},{16,0},{32,48},{48,32},{1,17},{17,1},{33,49},{49,33},{2,18}... | collective-permute-start | bytes 786440 | tf_op jit(solution)/shard_map/ppermute | solution.py:252
  56.9 13.4 %collective-permute-start.1 = (s16[16,2,16,256]{3,2,1,0:T(8,128)(2,1)S(1)}, s16[16,2,16,256]{3,2,1,0:T(8,128)(2,1)S(1)}, u32[]{:S(2)}, u32[]{:S(2)}) collective-permute-start(s16[16,2,16,256]{3,2,1,0:T(8,128)(2,1)S(1)} %get-tuple-element.12.refs_0_), channel_id=1, source_target_pairs={{0,32},{16,48},{32,0},{48,16},{1,33},{17,49},{33,1},{49,17},{2,34}... | collective-permute-start | bytes 786440 | tf_op jit(solution)/shard_map/ppermute | solution.py:252
  59.8 13.0 %collective-permute-start.2 = (s16[16,2,16,256]{3,2,1,0:T(8,128)(2,1)S(1)}, s16[16,2,16,256]{3,2,1,0:T(8,128)(2,1)S(1)}, u32[]{:S(2)}, u32[]{:S(2)}) collective-permute-start(s16[16,2,16,256]{3,2,1,0:T(8,128)(2,1)S(1)} %get-tuple-element.12.refs_0_), channel_id=1, source_target_pairs={{0,48},{16,32},{32,16},{48,0},{1,49},{17,33},{33,17},{49,1},{2,50}... | collective-permute-start | bytes 786440 | tf_op jit(solution)/shard_map/ppermute | solution.py:252
  60.1 12.8 %collective-permute-start.3 = (s16[16,2,16,256]{3,2,1,0:T(8,128)(2,1)S(1)}, s16[16,2,16,256]{3,2,1,0:T(8,128)(2,1)S(1)}, u32[]{:S(2)}, u32[]{:S(2)}) collective-permute-start(s16[16,2,16,256]{3,2,1,0:T(8,128)(2,1)S(1)} %get-tuple-element.13.refs_4_), channel_id=1, source_target_pairs={{0,64},{64,0},{128,192},{192,128},{1,65},{65,1},{129,193},{193,129... | collective-permute-start | bytes 786440 | tf_op jit(solution)/shard_map/ppermute | solution.py:252
  65.3 7.5 %collective-permute-start.5 = (s16[16,2,16,256]{3,2,1,0:T(8,128)(2,1)S(1)}, s16[16,2,16,256]{3,2,1,0:T(8,128)(2,1)S(1)}, u32[]{:S(2)}, u32[]{:S(2)}) collective-permute-start(s16[16,2,16,256]{3,2,1,0:T(8,128)(2,1)S(1)} %collective-permute-done.4.refs_6_), channel_id=1, source_target_pairs={{0,64},{64,0},{128,192},{192,128},{1,65},{65,1},{129,193},{193,129... | collective-permute-start | bytes 786440 | tf_op jit(solution)/shard_map/ppermute | solution.py:252
  74.9 16.4 %copy-start.1 = (bf16[96,64]{1,0:T(8,128)(2,1)S(1)}, bf16[96,64]{1,0:T(8,128)(2,1)}, u32[]{:S(2)}) copy-start(bf16[96,64]{1,0:T(8,128)(2,1)} %constant.22.clone.table_ref) | copy-start | bytes 36868
  92.9 18.4 %all-to-all-start.4 = ((s16[16,3,16,256]{3,2,1,0:T(8,128)(2,1)}), s16[16,3,16,256]{3,2,1,0:T(8,128)(2,1)S(1)}, u32[]{:S(2)}, u32[]{:S(2)}) async-start(s16[16,3,16,256]{3,2,1,0:T(8,128)(2,1)} %middle.1), calls=%async_computation.4 | async-start | bytes 786432 | tf_op jit(solution)/shard_map/all_to_all | solution.py:248
  97.2 13.1 %collective-permute-start.10 = (s16[16,3,16,256]{3,2,1,0:T(8,128)(2,1)S(1)}, s16[16,3,16,256]{3,2,1,0:T(8,128)(2,1)S(1)}, u32[]{:S(2)}, u32[]{:S(2)}) collective-permute-start(s16[16,3,16,256]{3,2,1,0:T(8,128)(2,1)S(1)} %get-tuple-element.17.refs_4_), channel_id=1, source_target_pairs={{0,128},{64,192},{128,0},{192,64},{1,129},{65,193},{129,1},{193,65... | collective-permute-start | bytes 1179656 | tf_op jit(solution)/shard_map/ppermute | solution.py:252
  99.3 12.0 %collective-permute-start.6 = (s16[16,3,16,256]{3,2,1,0:T(8,128)(2,1)S(1)}, s16[16,3,16,256]{3,2,1,0:T(8,128)(2,1)S(1)}, u32[]{:S(2)}, u32[]{:S(2)}) collective-permute-start(s16[16,3,16,256]{3,2,1,0:T(8,128)(2,1)S(1)} %get-tuple-element.16.refs_0_), channel_id=1, source_target_pairs={{0,16},{16,0},{32,48},{48,32},{1,17},{17,1},{33,49},{49,33},{2,18}... | collective-permute-start | bytes 1179656 | tf_op jit(solution)/shard_map/ppermute | solution.py:252
  99.3 19.0 %collective-permute-start.7 = (s16[16,3,16,256]{3,2,1,0:T(8,128)(2,1)S(1)}, s16[16,3,16,256]{3,2,1,0:T(8,128)(2,1)S(1)}, u32[]{:S(2)}, u32[]{:S(2)}) collective-permute-start(s16[16,3,16,256]{3,2,1,0:T(8,128)(2,1)S(1)} %get-tuple-element.16.refs_0_), channel_id=1, source_target_pairs={{0,32},{16,48},{32,0},{48,16},{1,33},{17,49},{33,1},{49,17},{2,34}... | collective-permute-start | bytes 1179656 | tf_op jit(solution)/shard_map/ppermute | solution.py:252
  102.2 18.7 %collective-permute-start.8 = (s16[16,3,16,256]{3,2,1,0:T(8,128)(2,1)S(1)}, s16[16,3,16,256]{3,2,1,0:T(8,128)(2,1)S(1)}, u32[]{:S(2)}, u32[]{:S(2)}) collective-permute-start(s16[16,3,16,256]{3,2,1,0:T(8,128)(2,1)S(1)} %get-tuple-element.16.refs_0_), channel_id=1, source_target_pairs={{0,48},{16,32},{32,16},{48,0},{1,49},{17,33},{33,17},{49,1},{2,50}... | collective-permute-start | bytes 1179656 | tf_op jit(solution)/shard_map/ppermute | solution.py:252
  104.0 16.9 %collective-permute-start.9 = (s16[16,3,16,256]{3,2,1,0:T(8,128)(2,1)S(1)}, s16[16,3,16,256]{3,2,1,0:T(8,128)(2,1)S(1)}, u32[]{:S(2)}, u32[]{:S(2)}) collective-permute-start(s16[16,3,16,256]{3,2,1,0:T(8,128)(2,1)S(1)} %get-tuple-element.17.refs_4_), channel_id=1, source_target_pairs={{0,64},{64,0},{128,192},{192,128},{1,65},{65,1},{129,193},{193,129... | collective-permute-start | bytes 1179656 | tf_op jit(solution)/shard_map/ppermute | solution.py:252
  110.3 10.6 %collective-permute-start.11 = (s16[16,3,16,256]{3,2,1,0:T(8,128)(2,1)S(1)}, s16[16,3,16,256]{3,2,1,0:T(8,128)(2,1)S(1)}, u32[]{:S(2)}, u32[]{:S(2)}) collective-permute-start(s16[16,3,16,256]{3,2,1,0:T(8,128)(2,1)S(1)} %collective-permute-done.10.refs_6_), channel_id=1, source_target_pairs={{0,64},{64,0},{128,192},{192,128},{1,65},{65,1},{129,193},{193,129... | collective-permute-start | bytes 1179656 | tf_op jit(solution)/shard_map/ppermute | solution.py:252
  111.3 17.3 %collective-permute-start.16 = (s16[16,3,16,256]{3,2,1,0:T(8,128)(2,1)S(1)}, s16[16,3,16,256]{3,2,1,0:T(8,128)(2,1)S(1)}, u32[]{:S(2)}, u32[]{:S(2)}) collective-permute-start(s16[16,3,16,256]{3,2,1,0:T(8,128)(2,1)S(1)} %all-to-all-done.4.refs_4_), channel_id=1, source_target_pairs={{0,128},{64,192},{128,0},{192,64},{1,129},{65,193},{129,1},{193,65... | collective-permute-start | bytes 1179656 | tf_op jit(solution)/shard_map/ppermute | solution.py:252
  123.8 10.5 %collective-permute-start.12 = (s16[16,3,16,256]{3,2,1,0:T(8,128)(2,1)S(1)}, s16[16,3,16,256]{3,2,1,0:T(8,128)(2,1)S(1)}, u32[]{:S(2)}, u32[]{:S(2)}) collective-permute-start(s16[16,3,16,256]{3,2,1,0:T(8,128)(2,1)S(1)} %shard_map.69.refs_0_), channel_id=1, source_target_pairs={{0,16},{16,0},{32,48},{48,32},{1,17},{17,1},{33,49},{49,33},{2,18}... | collective-permute-start | bytes 1179656 | tf_op jit(solution)/shard_map/ppermute | solution.py:252
  123.9 13.9 %collective-permute-start.13 = (s16[16,3,16,256]{3,2,1,0:T(8,128)(2,1)S(1)}, s16[16,3,16,256]{3,2,1,0:T(8,128)(2,1)S(1)}, u32[]{:S(2)}, u32[]{:S(2)}) collective-permute-start(s16[16,3,16,256]{3,2,1,0:T(8,128)(2,1)S(1)} %shard_map.69.refs_0_), channel_id=1, source_target_pairs={{0,32},{16,48},{32,0},{48,16},{1,33},{17,49},{33,1},{49,17},{2,34}... | collective-permute-start | bytes 1179656 | tf_op jit(solution)/shard_map/ppermute | solution.py:252
  125.6 15.2 %collective-permute-start.14 = (s16[16,3,16,256]{3,2,1,0:T(8,128)(2,1)S(1)}, s16[16,3,16,256]{3,2,1,0:T(8,128)(2,1)S(1)}, u32[]{:S(2)}, u32[]{:S(2)}) collective-permute-start(s16[16,3,16,256]{3,2,1,0:T(8,128)(2,1)S(1)} %shard_map.69.refs_0_), channel_id=1, source_target_pairs={{0,48},{16,32},{32,16},{48,0},{1,49},{17,33},{33,17},{49,1},{2,50}... | collective-permute-start | bytes 1179656 | tf_op jit(solution)/shard_map/ppermute | solution.py:252
  128.6 12.2 %collective-permute-start.15 = (s16[16,3,16,256]{3,2,1,0:T(8,128)(2,1)S(1)}, s16[16,3,16,256]{3,2,1,0:T(8,128)(2,1)S(1)}, u32[]{:S(2)}, u32[]{:S(2)}) collective-permute-start(s16[16,3,16,256]{3,2,1,0:T(8,128)(2,1)S(1)} %all-to-all-done.4.refs_4_), channel_id=1, source_target_pairs={{0,64},{64,0},{128,192},{192,128},{1,65},{65,1},{129,193},{193,129... | collective-permute-start | bytes 1179656 | tf_op jit(solution)/shard_map/ppermute | solution.py:252
  128.6 12.2 %collective-permute-start.17 = (s16[16,3,16,256]{3,2,1,0:T(8,128)(2,1)S(1)}, s16[16,3,16,256]{3,2,1,0:T(8,128)(2,1)S(1)}, u32[]{:S(2)}, u32[]{:S(2)}) collective-permute-start(s16[16,3,16,256]{3,2,1,0:T(8,128)(2,1)S(1)} %collective-permute-done.16.refs_6_), channel_id=1, source_target_pairs={{0,64},{64,0},{128,192},{192,128},{1,65},{65,1},{129,193},{193,129... | collective-permute-start | bytes 1179656 | tf_op jit(solution)/shard_map/ppermute | solution.py:252
  143.7 17.7 %copy-start = (bf16[96,96]{1,0:T(8,128)(2,1)S(1)}, bf16[96,96]{1,0:T(8,128)(2,1)}, u32[]{:S(2)}) copy-start(bf16[96,96]{1,0:T(8,128)(2,1)} %constant.23.clone.table_ref) | copy-start | bytes 55300

commit v3 on v2

--- a/solution.py
+++ b/solution.py
@@ -132,21 +132,28 @@
     out_ref[...] = value / float(modulus)
 
 
-def product_kernel(shift_ref, *refs):
-    left_refs, right_refs, out_ref = refs[:4], refs[4:8], refs[8]
-    shift = shift_ref[0]
+def product_kernel(row_ref, column_ref, *refs):
+    row, column = row_ref[0], column_ref[0]
+    ringed = len(refs) > 13
+    left_refs, right_refs, out_ref = refs[:-9], refs[-9:-5], refs[-5]
 
     def store_digits(piece, scratch, place):
-        high, low = digits_of(piece.reshape(256, 256))
+        high, low = digits_of(piece.reshape(-1, 256))
         for part, ref in zip((high, low), scratch):
             ref[place] = part
 
     for j in range(out_ref.shape[1]):
-        left_scratch, right_scratch = ([ref.at[j] for ref in refs[k : k + 2]] for k in (9, 11))
-        for m in range(4):
-            store_digits(left_refs[m][:, j], left_scratch, (slice(None), slice(256 * m, 256 * m + 256)))
-            block = pl.multiple_of((m ^ shift) * 256, 256)
-            store_digits(right_refs[m][:, j], right_scratch, (pl.ds(block, 256), slice(None)))
+        left_scratch, right_scratch = ([ref.at[j] for ref in group] for group in (refs[-4:-2], refs[-2:]))
+        done = 0
+        for ref in left_refs:
+            rows, block = 16 * ref.shape[0], 256 * (done // 256)
+            place = (slice(done % 256, done % 256 + rows), slice(block, block + 256))
+            store_digits(ref[:, j], left_scratch, place)
+            done += rows
+        for m, ref in enumerate(right_refs):
+            block = ((row ^ m) - column) & 3 if ringed else row ^ column ^ m
+            block = pl.multiple_of(block * 256, 256)
+            store_digits(ref[:, j], right_scratch, (pl.ds(block, 256), slice(None)))
         sums = [
             [jnp.dot(left[...], right[...], preferred_element_type=jnp.float32) for right in right_scratch]
             for left in left_scratch
@@ -156,6 +163,11 @@
         out_ref[:, j] = to_wire(value).reshape(16, 16, 256)
 
 
+def halves_kernel(first_ref, second_ref, low_ref, high_ref):
+    low_ref[...] = first_ref[...]
+    high_ref[...] = second_ref[...]
+
+
 def whole(shape):
     return pl.BlockSpec(shape, lambda i: (0,) * len(shape))
 
@@ -228,20 +240,35 @@
     )(table, values)
 
 
-def product(shift, left, right, aliases):
+def halves(first, second):
+    shape = (8,) + first.shape[1:]
+    half = lambda k: pl.BlockSpec(shape, lambda i: (k, 0, 0, 0))
+    return pl.pallas_call(
+        halves_kernel,
+        grid=(1,),
+        out_shape=[jax.ShapeDtypeStruct(shape, jnp.int16)] * 2,
+        in_specs=[half(0), half(1)],
+        out_specs=[whole(shape)] * 2,
+        compiler_params=params(4),
+        cost_estimate=cost(1 << 20),
+        name="halves",
+    )(first, second)
+
+
+def product(places, left, right, aliases):
     shape = left[0].shape
     return pl.pallas_call(
         product_kernel,
         grid=(1,),
         out_shape=jax.ShapeDtypeStruct(shape, jnp.int16),
-        in_specs=[pl.BlockSpec(memory_space=pltpu.SMEM)] + [whole(shape)] * 8,
+        in_specs=[pl.BlockSpec(memory_space=pltpu.SMEM)] * 2 + [whole(piece.shape) for piece in (*left, *right)],
         out_specs=whole(shape),
         scratch_shapes=[pltpu.VMEM((shape[1], 256, 1024), jnp.bfloat16)] * 2
         + [pltpu.VMEM((shape[1], 1024, 256), jnp.bfloat16)] * 2,
         input_output_aliases=aliases,
         compiler_params=params(20),
         cost_estimate=cost(shape[1] * 3 * 2 * 256 * 256 * 1024),
-    )(shift, *left, *right)
+    )(*places, *left, *right)
 
 
 def exchange(value):
@@ -254,6 +281,15 @@
 
 def along_columns(value):
     return [value] + [swapped(value, "col", m) for m in (1, 2, 3)]
+
+
+def round_columns(value):
+    def moved(piece, step):
+        return lax.ppermute(piece, "col", [(i, (i + step) % 4) for i in range(4)])
+
+    before, after = moved(value, 1), moved(value, 3)
+    low, high = halves(before, after)
+    return [value, after, moved(low, 1), moved(high, 3), before]
 
 
 def along_rows(value):
@@ -267,7 +303,7 @@
     spread_two = digit_table(forward_two[:, :DEG])
     lift = forward_two[:, :DEG] @ powers(2 * DEG, 2 * DEG, 2 * DEG, True)[DEG:] % modulus
     back = matrix_inverse(powers(4 * DEG, POINTS, POINTS))
-    shift = (lax.axis_index("row") ^ lax.axis_index("col")).astype(jnp.int32).reshape(1)
+    places = [lax.axis_index(axis).astype(jnp.int32).reshape(1) for axis in ("row", "col")]
 
     entries = exchange(pack(first_factors, second_factors))
     at_one = exchange(spread(spread_one, entries, 1))
@@ -276,15 +312,15 @@
     left_one, right_one = along_columns(left_one), along_rows(right_one)
     to_two, at_one = lax.optimization_barrier((to_two, at_one))
     at_two = exchange(to_two)
-    products_one = product(shift, left_one, right_one, {})
+    products_one = product(places, left_one, right_one, {})
     products_one, at_two = lax.optimization_barrier((products_one, at_two))
     returned = exchange(products_one)
     left_two, right_two = parted(at_two)
     left_two, right_two = along_columns(left_two), along_rows(right_two)
     to_lower = middle(digit_table(lift), returned)
-    upper = along_columns(product(shift, left_two, right_two, {1: 0}))
+    upper = round_columns(product(places, left_two, right_two, {2: 0}))
     lower = along_rows(exchange(to_lower))
-    products_two = exchange(product(shift, upper, lower, {1: 0}))
+    products_two = exchange(product(places, upper, lower, {2: 0}))
     return final(digit_table(back), products_two)
 
 

time: 164 us -> 167 us (1.018)
    ppermute x0 -> x4, waiting for transfers between devices: none -> 12.5 us  [moved(): return lax.ppermute(piece, 'col', [(i, (i + step) % 4) for i in range(4)])]
    ppermute x18 -> x15, waiting for transfers between devices: 40.3 us -> 28.6 us  [swapped(): return lax.ppermute(value, axis, [(i, i ^ bits) for i in range(4)])]
    ppermute x0 -> x4, starting transfers between devices: none -> 5.42 us  [moved(): return lax.ppermute(piece, 'col', [(i, (i + step) % 4) for i in range(4)])]
    ppermute x18 -> x15, starting transfers between devices: 20.8 us -> 16 us  [swapped(): return lax.ppermute(value, axis, [(i, i ^ bits) for i in range(4)])]
  transfers between devices with their start and end apart: 21 -> 22, of which waited for: 11 -> 11; matrix products, arithmetic and copies ran while one was open for 0% -> 0% of each run, Pallas kernels for 4% -> 5%
where the time goes in v3:
time: 167 us; the launch traced here: 165 us
  blocking collectives  57.8 us (35%)
  waiting for transfers between devices  53.8 us (32%)
  starting transfers between devices  36.2 us (22%)
  Pallas kernels  16.1 us (10%)
    all_to_all x3, blocking collectives, exchange(): return lax.all_to_all(value, 'pt', split_axis=0, concat_axis=0, tiled=True)  57.8 us
    ppermute x15, waiting for transfers between devices, swapped(): return lax.ppermute(value, axis, [(i, i ^ bits) for i in range(4)])  28.6 us
    ppermute x15, starting transfers between devices, swapped(): return lax.ppermute(value, axis, [(i, i ^ bits) for i in range(4)])  16 us
    all_to_all x3, starting transfers between devices, exchange(): return lax.all_to_all(value, 'pt', split_axis=0, concat_axis=0, tiled=True)  14.8 us
    all_to_all x3, waiting for transfers between devices, exchange(): return lax.all_to_all(value, 'pt', split_axis=0, concat_axis=0, tiled=True)  12.7 us
    ppermute x4, waiting for transfers between devices, moved(): return lax.ppermute(piece, 'col', [(i, (i + step) % 4) for i in range(4)])  12.5 us
    pallas_call x3, Pallas kernels, product(): pl.pallas_call(product_kernel, grid=(1,), out_shape=jax.ShapeDtypeStruct(...  8.64 us
    ppermute x4, starting transfers between devices, moved(): return lax.ppermute(piece, 'col', [(i, (i + step) % 4) for i in range(4)])  5.42 us
  transfers between devices with their start and end apart: 22, of which 11 were waited for; matrix products, arithmetic and copies ran while one was open for 0% of the time, Pallas kernels for 5%

profile of v3, /device:TPU:32, one launch (start us, length us, event | category | flops | bytes accessed | tf_op | source)
XLA Modules:
  0.0 165.2 jit_solution(2604877546745889535)
XLA Ops:
  0.0 1.1 add_convert_fusion.1
  1.1 0.1 copy-done.4
  1.2 0.1 copy_bitcast_fusion
  1.3 0.0 copy-start.3
  1.3 24.3 %all_to_all.30.in_ref = s16[16,2,2,16,256]{4,3,2,1,0:T(8,128)(2,1)S(1)} all-to-all(s16[16,2,2,16,256]{4,3,2,1,0:T(8,128)(2,1)S(1)} %copy_bitcast_fusion), channel_id=1, replica_groups=mesh['row'=4,'col'=4,'pt'=16] {'pt'}, dimensions={0} | all-to-all | bytes 1048576 | tf_op jit(solution)/shard_map/all_to_all | solution.py:275
  25.6 1.6 shard_map.64
  27.2 5.4 %all-to-all-start.1 = ((s16[16,4,16,256]{3,2,1,0:T(8,128)(2,1)}), s16[16,4,16,256]{3,2,1,0:T(8,128)(2,1)S(1)}, u32[]{:S(2)}, u32[]{:S(2)}) async-start(s16[16,4,16,256]{3,2,1,0:T(8,128)(2,1)} %shard_map.64), calls=%async_computation.1 | async-start | bytes 1048576 | tf_op jit(solution)/shard_map/all_to_all | solution.py:275
  32.6 2.0 %shard_map.67 = s16[16,6,16,256]{3,2,1,0:T(8,128)(2,1)} custom-call(bf16[96,32]{1,0:T(8,128)(2,1)S(1)} %copy-done.2, s16[16,2,2,16,256]{4,3,2,1,0:T(8,128)(2,1)S(1)} %all_to_all.30.in_ref), custom_call_target="tpu_custom_call" | custom-call | flops 50331648 | bytes 65536 | tf_op jit(solution)/shard_map/pallas_call | solution.py:204
  34.6 12.7 %all-to-all-done.1.in_ref = s16[16,4,16,256]{3,2,1,0:T(8,128)(2,1)S(1)} async-done(((s16[16,4,16,256]{3,2,1,0:T(8,128)(2,1)}), s16[16,4,16,256]{3,2,1,0:T(8,128)(2,1)S(1)}, u32[]{:S(2)}, u32[]{:S(2)}) %all-to-all-start.1) | async-done | bytes 524320 | tf_op jit(solution)/shard_map/all_to_all | solution.py:275
  47.3 5.2 %all-to-all-start.2 = ((s16[16,6,16,256]{3,2,1,0:T(8,128)(2,1)}), s16[16,6,16,256]{3,2,1,0:T(8,128)(2,1)S(1)}, u32[]{:S(2)}, u32[]{:S(2)}) async-start(s16[16,6,16,256]{3,2,1,0:T(8,128)(2,1)} %shard_map.67), calls=%async_computation.2 | async-start | bytes 1572864 | tf_op jit(solution)/shard_map/all_to_all | solution.py:275
  52.5 2.8 %collective-permute-start.4 = (s16[16,2,16,256]{3,2,1,0:T(8,128)(2,1)S(1)}, s16[16,2,16,256]{3,2,1,0:T(8,128)(2,1)S(1)}, u32[]{:S(2)}, u32[]{:S(2)}) collective-permute-start(s16[16,2,16,256]{3,2,1,0:T(8,128)(2,1)S(1)} %get-tuple-element.15.refs_4_), channel_id=1, source_target_pairs={{0,128},{64,192},{128,0},{192,64},{1,129},{65,193},{129,1},{193,65... | collective-permute-start | bytes 786440 | tf_op jit(solution)/shard_map/ppermute | solution.py:279
  55.4 1.6 collective-permute-start
  56.9 2.9 %collective-permute-start.1 = (s16[16,2,16,256]{3,2,1,0:T(8,128)(2,1)S(1)}, s16[16,2,16,256]{3,2,1,0:T(8,128)(2,1)S(1)}, u32[]{:S(2)}, u32[]{:S(2)}) collective-permute-start(s16[16,2,16,256]{3,2,1,0:T(8,128)(2,1)S(1)} %get-tuple-element.14.refs_0_), channel_id=1, source_target_pairs={{0,32},{16,48},{32,0},{48,16},{1,33},{17,49},{33,1},{49,17},{2,34}... | collective-permute-start | bytes 786440 | tf_op jit(solution)/shard_map/ppermute | solution.py:279
  59.8 0.2 collective-permute-start.2
  60.1 5.3 %collective-permute-done.4.refs_6_ = s16[16,2,16,256]{3,2,1,0:T(8,128)(2,1)S(1)} collective-permute-done((s16[16,2,16,256]{3,2,1,0:T(8,128)(2,1)S(1)}, s16[16,2,16,256]{3,2,1,0:T(8,128)(2,1)S(1)}, u32[]{:S(2)}, u32[]{:S(2)}) %collective-permute-start.4) | collective-permute-done | bytes 262176 | tf_op jit(solution)/shard_map/ppermute | solution.py:279
  65.3 0.0 collective-permute-start.5
  65.3 0.0 collective-permute-done.refs_1_
  65.3 5.0 %collective-permute-done.1.refs_2_ = s16[16,2,16,256]{3,2,1,0:T(8,128)(2,1)S(1)} collective-permute-done((s16[16,2,16,256]{3,2,1,0:T(8,128)(2,1)S(1)}, s16[16,2,16,256]{3,2,1,0:T(8,128)(2,1)S(1)}, u32[]{:S(2)}, u32[]{:S(2)}) %collective-permute-start.1) | collective-permute-done | bytes 262176 | tf_op jit(solution)/shard_map/ppermute | solution.py:279
  70.3 2.6 %collective-permute-done.2.refs_3_ = s16[16,2,16,256]{3,2,1,0:T(8,128)(2,1)S(1)} collective-permute-done((s16[16,2,16,256]{3,2,1,0:T(8,128)(2,1)S(1)}, s16[16,2,16,256]{3,2,1,0:T(8,128)(2,1)S(1)}, u32[]{:S(2)}, u32[]{:S(2)}) %collective-permute-start.2) | collective-permute-done | bytes 262176 | tf_op jit(solution)/shard_map/ppermute | solution.py:279
  72.9 2.0 %shard_map.66 = s16[16,2,16,256]{3,2,1,0:T(8,128)(2,1)S(1)} custom-call(s32[1]{0:T(128)} %bitcast.row_ref, s32[1]{0:T(128)} %bitcast.1.column_ref, s16[16,2,16,256]{3,2,1,0:T(8,128)(2,1)S(1)} %get-tuple-element.14.refs_0_, s16[16,2,16,256]{3,2,1,0:T(8,128)(2,1)S(1)} %collective-permute-done.refs_1_, ...), custom_call_target="tpu_custom_call" | custom-call | flops 100663296 | bytes 65536 | tf_op jit(solution)/shard_map/pallas_call | solution.py:260
  74.9 0.0 copy-start.1
  74.9 16.4 %all_to_all.31.in_ref = s16[16,2,16,256]{3,2,1,0:T(8,128)(2,1)S(1)} all-to-all(s16[16,2,16,256]{3,2,1,0:T(8,128)(2,1)S(1)} %shard_map.66), channel_id=1, replica_groups=mesh['row'=4,'col'=4,'pt'=16] {'pt'}, dimensions={0} | all-to-all | bytes 524288 | tf_op jit(solution)/shard_map/all_to_all | solution.py:275
  91.2 1.7 %middle.1 = s16[16,3,16,256]{3,2,1,0:T(8,128)(2,1)} custom-call(bf16[96,64]{1,0:T(8,128)(2,1)S(1)} %copy-done.1, s16[16,2,16,256]{3,2,1,0:T(8,128)(2,1)S(1)} %all_to_all.31.in_ref), custom_call_target="tpu_custom_call" | custom-call | flops 50331648 | bytes 65536 | tf_op jit(solution)/shard_map/middle/pallas_call | solution.py:217
  92.9 4.2 %all-to-all-start.4 = ((s16[16,3,16,256]{3,2,1,0:T(8,128)(2,1)}), s16[16,3,16,256]{3,2,1,0:T(8,128)(2,1)S(1)}, u32[]{:S(2)}, u32[]{:S(2)}) async-start(s16[16,3,16,256]{3,2,1,0:T(8,128)(2,1)} %middle.1), calls=%async_computation.4 | async-start | bytes 786432 | tf_op jit(solution)/shard_map/all_to_all | solution.py:275
  97.1 0.1 shard_map.68
  97.2 2.1 %collective-permute-start.10 = (s16[16,3,16,256]{3,2,1,0:T(8,128)(2,1)S(1)}, s16[16,3,16,256]{3,2,1,0:T(8,128)(2,1)S(1)}, u32[]{:S(2)}, u32[]{:S(2)}) collective-permute-start(s16[16,3,16,256]{3,2,1,0:T(8,128)(2,1)S(1)} %get-tuple-element.19.refs_4_), channel_id=1, source_target_pairs={{0,128},{64,192},{128,0},{192,64},{1,129},{65,193},{129,1},{193,65... | collective-permute-start | bytes 1179656 | tf_op jit(solution)/shard_map/ppermute | solution.py:279
  99.3 0.0 collective-permute-start.6
  99.3 2.9 %collective-permute-start.7 = (s16[16,3,16,256]{3,2,1,0:T(8,128)(2,1)S(1)}, s16[16,3,16,256]{3,2,1,0:T(8,128)(2,1)S(1)}, u32[]{:S(2)}, u32[]{:S(2)}) collective-permute-start(s16[16,3,16,256]{3,2,1,0:T(8,128)(2,1)S(1)} %get-tuple-element.18.refs_0_), channel_id=1, source_target_pairs={{0,32},{16,48},{32,0},{48,16},{1,33},{17,49},{33,1},{49,17},{2,34}... | collective-permute-start | bytes 1179656 | tf_op jit(solution)/shard_map/ppermute | solution.py:279
  102.2 1.8 %collective-permute-start.8 = (s16[16,3,16,256]{3,2,1,0:T(8,128)(2,1)S(1)}, s16[16,3,16,256]{3,2,1,0:T(8,128)(2,1)S(1)}, u32[]{:S(2)}, u32[]{:S(2)}) collective-permute-start(s16[16,3,16,256]{3,2,1,0:T(8,128)(2,1)S(1)} %get-tuple-element.18.refs_0_), channel_id=1, source_target_pairs={{0,48},{16,32},{32,16},{48,0},{1,49},{17,33},{33,17},{49,1},{2,50}... | collective-permute-start | bytes 1179656 | tf_op jit(solution)/shard_map/ppermute | solution.py:279
  104.0 6.3 %collective-permute-done.10.refs_6_ = s16[16,3,16,256]{3,2,1,0:T(8,128)(2,1)S(1)} collective-permute-done((s16[16,3,16,256]{3,2,1,0:T(8,128)(2,1)S(1)}, s16[16,3,16,256]{3,2,1,0:T(8,128)(2,1)S(1)}, u32[]{:S(2)}, u32[]{:S(2)}) %collective-permute-start.10) | collective-permute-done | bytes 393248 | tf_op jit(solution)/shard_map/ppermute | solution.py:279
  110.3 0.0 collective-permute-start.11
  110.3 1.0 collective-permute-done.6.refs_1_
  111.3 1.2 collective-permute-start.17
  112.4 5.9 %collective-permute-done.7.refs_2_ = s16[16,3,16,256]{3,2,1,0:T(8,128)(2,1)S(1)} collective-permute-done((s16[16,3,16,256]{3,2,1,0:T(8,128)(2,1)S(1)}, s16[16,3,16,256]{3,2,1,0:T(8,128)(2,1)S(1)}, u32[]{:S(2)}, u32[]{:S(2)}) %collective-permute-start.7) | collective-permute-done | bytes 393248 | tf_op jit(solution)/shard_map/ppermute | solution.py:279
  118.3 2.6 %collective-permute-done.8.refs_3_ = s16[16,3,16,256]{3,2,1,0:T(8,128)(2,1)S(1)} collective-permute-done((s16[16,3,16,256]{3,2,1,0:T(8,128)(2,1)S(1)}, s16[16,3,16,256]{3,2,1,0:T(8,128)(2,1)S(1)}, u32[]{:S(2)}, u32[]{:S(2)}) %collective-permute-start.8) | collective-permute-done | bytes 393248 | tf_op jit(solution)/shard_map/ppermute | solution.py:279
  120.9 3.9 %shard_map.69.refs_0_ = s16[16,3,16,256]{3,2,1,0:T(8,128)(2,1)S(1)} custom-call(s32[1]{0:T(128)} %bitcast.row_ref, s32[1]{0:T(128)} %bitcast.1.column_ref, s16[16,3,16,256]{3,2,1,0:T(8,128)(2,1)S(1)} %get-tuple-element.18.refs_0_, s16[16,3,16,256]{3,2,1,0:T(8,128)(2,1)S(1)} %collective-permute-done.6.refs_1_, ...), custom_call_target="tpu_custom_call", output_to_operand_aliasing={{}: (2, {})} | custom-call | flops 150994944 | bytes 65536 | tf_op jit(solution)/shard_map/pallas_call | solution.py:260
  124.8 0.4 collective-permute-start.12
  125.2 1.7 %collective-permute-start.13 = (s16[16,3,16,256]{3,2,1,0:T(8,128)(2,1)S(1)}, s16[16,3,16,256]{3,2,1,0:T(8,128)(2,1)S(1)}, u32[]{:S(2)}, u32[]{:S(2)}) collective-permute-start(s16[16,3,16,256]{3,2,1,0:T(8,128)(2,1)S(1)} %shard_map.69.refs_0_), channel_id=1, source_target_pairs={{0,16},{16,32},{32,48},{48,0},{1,17},{17,33},{33,49},{49,1},{2,18}... | collective-permute-start | bytes 1179656 | tf_op jit(solution)/shard_map/ppermute | solution.py:288
  126.9 0.5 collective-permute-start.18
  127.4 6.8 %collective-permute-done.12.second_ref.refs_1_ = s16[16,3,16,256]{3,2,1,0:T(8,128)(2,1)S(1)} collective-permute-done((s16[16,3,16,256]{3,2,1,0:T(8,128)(2,1)S(1)}, s16[16,3,16,256]{3,2,1,0:T(8,128)(2,1)S(1)}, u32[]{:S(2)}, u32[]{:S(2)}) %collective-permute-start.12) | collective-permute-done | bytes 393248 | tf_op jit(solution)/shard_map/ppermute | solution.py:288
  134.2 2.0 %collective-permute-done.13.first_ref.refs_4_ = s16[16,3,16,256]{3,2,1,0:T(8,128)(2,1)S(1)} collective-permute-done((s16[16,3,16,256]{3,2,1,0:T(8,128)(2,1)S(1)}, s16[16,3,16,256]{3,2,1,0:T(8,128)(2,1)S(1)}, u32[]{:S(2)}, u32[]{:S(2)}) %collective-permute-start.13) | collective-permute-done | bytes 393248 | tf_op jit(solution)/shard_map/ppermute | solution.py:288
  136.3 0.6 collective-permute-start.14
  136.9 2.7 %collective-permute-start.15 = (s16[8,3,16,256]{3,2,1,0:T(8,128)(2,1)S(1)}, s16[8,3,16,256]{3,2,1,0:T(8,128)(2,1)S(1)}, u32[]{:S(2)}, u32[]{:S(2)}) collective-permute-start(s16[8,3,16,256]{3,2,1,0:T(8,128)(2,1)S(1)} %get-tuple-element.21), channel_id=1, source_target_pairs={{0,48},{16,0},{32,16},{48,32},{1,49},{17,1},{33,17},{49,33},{2,50}... | collective-permute-start | bytes 589832 | tf_op jit(solution)/shard_map/ppermute | solution.py:288
  139.6 3.6 %collective-permute-done.14.refs_2_ = s16[8,3,16,256]{3,2,1,0:T(8,128)(2,1)S(1)} collective-permute-done((s16[8,3,16,256]{3,2,1,0:T(8,128)(2,1)S(1)}, s16[8,3,16,256]{3,2,1,0:T(8,128)(2,1)S(1)}, u32[]{:S(2)}, u32[]{:S(2)}) %collective-permute-start.14) | collective-permute-done | bytes 196640 | tf_op jit(solution)/shard_map/ppermute | solution.py:288
  143.3 2.8 %shard_map.70 = s16[16,3,16,256]{3,2,1,0:T(8,128)(2,1)S(1)} custom-call(s32[1]{0:T(128)} %bitcast.row_ref, s32[1]{0:T(128)} %bitcast.1.column_ref, s16[16,3,16,256]{3,2,1,0:T(8,128)(2,1)S(1)} %shard_map.69.refs_0_, s16[16,3,16,256]{3,2,1,0:T(8,128)(2,1)S(1)} %collective-permute-done.12.second_ref.refs_1_, ...), custom_call_target="tpu_custom_call", output_to_operand_aliasing={{}: (2, {})} | custom-call | flops 150994944 | bytes 65536 | tf_op jit(solution)/shard_map/pallas_call | solution.py:260
  146.0 0.0 copy-start
  146.1 17.2 %all_to_all.32.in_ref = s16[16,3,16,256]{3,2,1,0:T(8,128)(2,1)S(1)} all-to-all(s16[16,3,16,256]{3,2,1,0:T(8,128)(2,1)S(1)} %shard_map.70), channel_id=1, replica_groups=mesh['row'=4,'col'=4,'pt'=16] {'pt'}, dimensions={0} | all-to-all | bytes 786432 | tf_op jit(solution)/shard_map/all_to_all | solution.py:275
  163.2 2.0 %final.1 = f32[45,16,256]{2,1,0:T(8,128)} custom-call(bf16[96,96]{1,0:T(8,128)(2,1)S(1)} %copy-done, s16[16,3,16,256]{3,2,1,0:T(8,128)(2,1)S(1)} %all_to_all.32.in_ref), custom_call_target="tpu_custom_call" | custom-call | flops 75497472 | bytes 65536 | tf_op jit(solution)/shard_map/final/pallas_call | solution.py:231
  (22 shorter events, 0.1 us)
Async XLA Ops:
  0.0 1.2 copy-start.4
  1.3 24.3 %copy-start.3 = (bf16[64,32]{1,0:T(8,128)(2,1)S(1)}, bf16[64,32]{1,0:T(8,128)(2,1)}, u32[]{:S(2)}) copy-start(bf16[64,32]{1,0:T(8,128)(2,1)} %constant.20.clone.table_ref) | copy-start | bytes 12292
  27.2 5.4 %copy-start.2 = (bf16[96,32]{1,0:T(8,128)(2,1)S(1)}, bf16[96,32]{1,0:T(8,128)(2,1)}, u32[]{:S(2)}) copy-start(bf16[96,32]{1,0:T(8,128)(2,1)} %constant.21.clone.table_ref) | copy-start | bytes 18436
  27.2 20.1 %all-to-all-start.1 = ((s16[16,4,16,256]{3,2,1,0:T(8,128)(2,1)}), s16[16,4,16,256]{3,2,1,0:T(8,128)(2,1)S(1)}, u32[]{:S(2)}, u32[]{:S(2)}) async-start(s16[16,4,16,256]{3,2,1,0:T(8,128)(2,1)} %shard_map.64), calls=%async_computation.1 | async-start | bytes 1048576 | tf_op jit(solution)/shard_map/all_to_all | solution.py:275
  47.3 27.5 %all-to-all-start.2 = ((s16[16,6,16,256]{3,2,1,0:T(8,128)(2,1)}), s16[16,6,16,256]{3,2,1,0:T(8,128)(2,1)S(1)}, u32[]{:S(2)}, u32[]{:S(2)}) async-start(s16[16,6,16,256]{3,2,1,0:T(8,128)(2,1)} %shard_map.67), calls=%async_computation.2 | async-start | bytes 1572864 | tf_op jit(solution)/shard_map/all_to_all | solution.py:275
  52.5 12.8 %collective-permute-start.4 = (s16[16,2,16,256]{3,2,1,0:T(8,128)(2,1)S(1)}, s16[16,2,16,256]{3,2,1,0:T(8,128)(2,1)S(1)}, u32[]{:S(2)}, u32[]{:S(2)}) collective-permute-start(s16[16,2,16,256]{3,2,1,0:T(8,128)(2,1)S(1)} %get-tuple-element.15.refs_4_), channel_id=1, source_target_pairs={{0,128},{64,192},{128,0},{192,64},{1,129},{65,193},{129,1},{193,65... | collective-permute-start | bytes 786440 | tf_op jit(solution)/shard_map/ppermute | solution.py:279
  55.4 10.0 %collective-permute-start = (s16[16,2,16,256]{3,2,1,0:T(8,128)(2,1)S(1)}, s16[16,2,16,256]{3,2,1,0:T(8,128)(2,1)S(1)}, u32[]{:S(2)}, u32[]{:S(2)}) collective-permute-start(s16[16,2,16,256]{3,2,1,0:T(8,128)(2,1)S(1)} %get-tuple-element.14.refs_0_), channel_id=1, source_target_pairs={{0,16},{16,0},{32,48},{48,32},{1,17},{17,1},{33,49},{49,33},{2,18}... | collective-permute-start | bytes 786440 | tf_op jit(solution)/shard_map/ppermute | solution.py:279
  56.9 13.4 %collective-permute-start.1 = (s16[16,2,16,256]{3,2,1,0:T(8,128)(2,1)S(1)}, s16[16,2,16,256]{3,2,1,0:T(8,128)(2,1)S(1)}, u32[]{:S(2)}, u32[]{:S(2)}) collective-permute-start(s16[16,2,16,256]{3,2,1,0:T(8,128)(2,1)S(1)} %get-tuple-element.14.refs_0_), channel_id=1, source_target_pairs={{0,32},{16,48},{32,0},{48,16},{1,33},{17,49},{33,1},{49,17},{2,34}... | collective-permute-start | bytes 786440 | tf_op jit(solution)/shard_map/ppermute | solution.py:279
  59.8 13.0 %collective-permute-start.2 = (s16[16,2,16,256]{3,2,1,0:T(8,128)(2,1)S(1)}, s16[16,2,16,256]{3,2,1,0:T(8,128)(2,1)S(1)}, u32[]{:S(2)}, u32[]{:S(2)}) collective-permute-start(s16[16,2,16,256]{3,2,1,0:T(8,128)(2,1)S(1)} %get-tuple-element.14.refs_0_), channel_id=1, source_target_pairs={{0,48},{16,32},{32,16},{48,0},{1,49},{17,33},{33,17},{49,1},{2,50}... | collective-permute-start | bytes 786440 | tf_op jit(solution)/shard_map/ppermute | solution.py:279
  60.1 12.8 %collective-permute-start.3 = (s16[16,2,16,256]{3,2,1,0:T(8,128)(2,1)S(1)}, s16[16,2,16,256]{3,2,1,0:T(8,128)(2,1)S(1)}, u32[]{:S(2)}, u32[]{:S(2)}) collective-permute-start(s16[16,2,16,256]{3,2,1,0:T(8,128)(2,1)S(1)} %get-tuple-element.15.refs_4_), channel_id=1, source_target_pairs={{0,64},{64,0},{128,192},{192,128},{1,65},{65,1},{129,193},{193,129... | collective-permute-start | bytes 786440 | tf_op jit(solution)/shard_map/ppermute | solution.py:279
  65.3 7.5 %collective-permute-start.5 = (s16[16,2,16,256]{3,2,1,0:T(8,128)(2,1)S(1)}, s16[16,2,16,256]{3,2,1,0:T(8,128)(2,1)S(1)}, u32[]{:S(2)}, u32[]{:S(2)}) collective-permute-start(s16[16,2,16,256]{3,2,1,0:T(8,128)(2,1)S(1)} %collective-permute-done.4.refs_6_), channel_id=1, source_target_pairs={{0,64},{64,0},{128,192},{192,128},{1,65},{65,1},{129,193},{193,129... | collective-permute-start | bytes 786440 | tf_op jit(solution)/shard_map/ppermute | solution.py:279
  74.9 16.4 %copy-start.1 = (bf16[96,64]{1,0:T(8,128)(2,1)S(1)}, bf16[96,64]{1,0:T(8,128)(2,1)}, u32[]{:S(2)}) copy-start(bf16[96,64]{1,0:T(8,128)(2,1)} %constant.22.clone.table_ref) | copy-start | bytes 36868
  92.9 18.3 %all-to-all-start.4 = ((s16[16,3,16,256]{3,2,1,0:T(8,128)(2,1)}), s16[16,3,16,256]{3,2,1,0:T(8,128)(2,1)S(1)}, u32[]{:S(2)}, u32[]{:S(2)}) async-start(s16[16,3,16,256]{3,2,1,0:T(8,128)(2,1)} %middle.1), calls=%async_computation.4 | async-start | bytes 786432 | tf_op jit(solution)/shard_map/all_to_all | solution.py:275
  97.2 13.1 %collective-permute-start.10 = (s16[16,3,16,256]{3,2,1,0:T(8,128)(2,1)S(1)}, s16[16,3,16,256]{3,2,1,0:T(8,128)(2,1)S(1)}, u32[]{:S(2)}, u32[]{:S(2)}) collective-permute-start(s16[16,3,16,256]{3,2,1,0:T(8,128)(2,1)S(1)} %get-tuple-element.19.refs_4_), channel_id=1, source_target_pairs={{0,128},{64,192},{128,0},{192,64},{1,129},{65,193},{129,1},{193,65... | collective-permute-start | bytes 1179656 | tf_op jit(solution)/shard_map/ppermute | solution.py:279
  99.3 12.0 %collective-permute-start.6 = (s16[16,3,16,256]{3,2,1,0:T(8,128)(2,1)S(1)}, s16[16,3,16,256]{3,2,1,0:T(8,128)(2,1)S(1)}, u32[]{:S(2)}, u32[]{:S(2)}) collective-permute-start(s16[16,3,16,256]{3,2,1,0:T(8,128)(2,1)S(1)} %get-tuple-element.18.refs_0_), channel_id=1, source_target_pairs={{0,16},{16,0},{32,48},{48,32},{1,17},{17,1},{33,49},{49,33},{2,18}... | collective-permute-start | bytes 1179656 | tf_op jit(solution)/shard_map/ppermute | solution.py:279
  99.3 19.0 %collective-permute-start.7 = (s16[16,3,16,256]{3,2,1,0:T(8,128)(2,1)S(1)}, s16[16,3,16,256]{3,2,1,0:T(8,128)(2,1)S(1)}, u32[]{:S(2)}, u32[]{:S(2)}) collective-permute-start(s16[16,3,16,256]{3,2,1,0:T(8,128)(2,1)S(1)} %get-tuple-element.18.refs_0_), channel_id=1, source_target_pairs={{0,32},{16,48},{32,0},{48,16},{1,33},{17,49},{33,1},{49,17},{2,34}... | collective-permute-start | bytes 1179656 | tf_op jit(solution)/shard_map/ppermute | solution.py:279
  102.2 18.7 %collective-permute-start.8 = (s16[16,3,16,256]{3,2,1,0:T(8,128)(2,1)S(1)}, s16[16,3,16,256]{3,2,1,0:T(8,128)(2,1)S(1)}, u32[]{:S(2)}, u32[]{:S(2)}) collective-permute-start(s16[16,3,16,256]{3,2,1,0:T(8,128)(2,1)S(1)} %get-tuple-element.18.refs_0_), channel_id=1, source_target_pairs={{0,48},{16,32},{32,16},{48,0},{1,49},{17,33},{33,17},{49,1},{2,50}... | collective-permute-start | bytes 1179656 | tf_op jit(solution)/shard_map/ppermute | solution.py:279
  104.0 16.9 %collective-permute-start.9 = (s16[16,3,16,256]{3,2,1,0:T(8,128)(2,1)S(1)}, s16[16,3,16,256]{3,2,1,0:T(8,128)(2,1)S(1)}, u32[]{:S(2)}, u32[]{:S(2)}) collective-permute-start(s16[16,3,16,256]{3,2,1,0:T(8,128)(2,1)S(1)} %get-tuple-element.19.refs_4_), channel_id=1, source_target_pairs={{0,64},{64,0},{128,192},{192,128},{1,65},{65,1},{129,193},{193,129... | collective-permute-start | bytes 1179656 | tf_op jit(solution)/shard_map/ppermute | solution.py:279
  110.3 10.6 %collective-permute-start.11 = (s16[16,3,16,256]{3,2,1,0:T(8,128)(2,1)S(1)}, s16[16,3,16,256]{3,2,1,0:T(8,128)(2,1)}, u32[]{:S(2)}, u32[]{:S(2)}) collective-permute-start(s16[16,3,16,256]{3,2,1,0:T(8,128)(2,1)S(1)} %collective-permute-done.10.refs_6_), channel_id=1, source_target_pairs={{0,64},{64,0},{128,192},{192,128},{1,65},{65,1},{129,193},{193,129... | collective-permute-start | bytes 1179656 | tf_op jit(solution)/shard_map/ppermute | solution.py:279
  111.3 15.6 %collective-permute-start.17 = (s16[16,3,16,256]{3,2,1,0:T(8,128)(2,1)S(1)}, s16[16,3,16,256]{3,2,1,0:T(8,128)(2,1)S(1)}, u32[]{:S(2)}, u32[]{:S(2)}) collective-permute-start(s16[16,3,16,256]{3,2,1,0:T(8,128)(2,1)S(1)} %all-to-all-done.4.refs_5_), channel_id=1, source_target_pairs={{0,128},{64,192},{128,0},{192,64},{1,129},{65,193},{129,1},{193,65... | collective-permute-start | bytes 1179656 | tf_op jit(solution)/shard_map/ppermute | solution.py:279
  124.8 9.5 %collective-permute-start.12 = (s16[16,3,16,256]{3,2,1,0:T(8,128)(2,1)S(1)}, s16[16,3,16,256]{3,2,1,0:T(8,128)(2,1)S(1)}, u32[]{:S(2)}, u32[]{:S(2)}) collective-permute-start(s16[16,3,16,256]{3,2,1,0:T(8,128)(2,1)S(1)} %shard_map.69.refs_0_), channel_id=1, source_target_pairs={{0,48},{16,0},{32,16},{48,32},{1,49},{17,1},{33,17},{49,33},{2,50}... | collective-permute-start | bytes 1179656 | tf_op jit(solution)/shard_map/ppermute | solution.py:288
  125.2 11.1 %collective-permute-start.13 = (s16[16,3,16,256]{3,2,1,0:T(8,128)(2,1)S(1)}, s16[16,3,16,256]{3,2,1,0:T(8,128)(2,1)S(1)}, u32[]{:S(2)}, u32[]{:S(2)}) collective-permute-start(s16[16,3,16,256]{3,2,1,0:T(8,128)(2,1)S(1)} %shard_map.69.refs_0_), channel_id=1, source_target_pairs={{0,16},{16,32},{32,48},{48,0},{1,17},{17,33},{33,49},{49,1},{2,18}... | collective-permute-start | bytes 1179656 | tf_op jit(solution)/shard_map/ppermute | solution.py:288
  126.9 16.3 %collective-permute-start.16 = (s16[16,3,16,256]{3,2,1,0:T(8,128)(2,1)S(1)}, s16[16,3,16,256]{3,2,1,0:T(8,128)(2,1)S(1)}, u32[]{:S(2)}, u32[]{:S(2)}) collective-permute-start(s16[16,3,16,256]{3,2,1,0:T(8,128)(2,1)S(1)} %all-to-all-done.4.refs_5_), channel_id=1, source_target_pairs={{0,64},{64,0},{128,192},{192,128},{1,65},{65,1},{129,193},{193,129... | collective-permute-start | bytes 1179656 | tf_op jit(solution)/shard_map/ppermute | solution.py:279
  126.9 16.3 %collective-permute-start.18 = (s16[16,3,16,256]{3,2,1,0:T(8,128)(2,1)S(1)}, s16[16,3,16,256]{3,2,1,0:T(8,128)(2,1)S(1)}, u32[]{:S(2)}, u32[]{:S(2)}) collective-permute-start(s16[16,3,16,256]{3,2,1,0:T(8,128)(2,1)S(1)} %collective-permute-done.17.refs_7_), channel_id=1, source_target_pairs={{0,64},{64,0},{128,192},{192,128},{1,65},{65,1},{129,193},{193,129... | collective-permute-start | bytes 1179656 | tf_op jit(solution)/shard_map/ppermute | solution.py:279
  136.3 7.0 %collective-permute-start.14 = (s16[8,3,16,256]{3,2,1,0:T(8,128)(2,1)S(1)}, s16[8,3,16,256]{3,2,1,0:T(8,128)(2,1)S(1)}, u32[]{:S(2)}, u32[]{:S(2)}) collective-permute-start(s16[8,3,16,256]{3,2,1,0:T(8,128)(2,1)S(1)} %get-tuple-element.20), channel_id=1, source_target_pairs={{0,16},{16,32},{32,48},{48,0},{1,17},{17,33},{33,49},{49,1},{2,18}... | collective-permute-start | bytes 589832 | tf_op jit(solution)/shard_map/ppermute | solution.py:288
  136.9 6.4 %collective-permute-start.15 = (s16[8,3,16,256]{3,2,1,0:T(8,128)(2,1)S(1)}, s16[8,3,16,256]{3,2,1,0:T(8,128)(2,1)S(1)}, u32[]{:S(2)}, u32[]{:S(2)}) collective-permute-start(s16[8,3,16,256]{3,2,1,0:T(8,128)(2,1)S(1)} %get-tuple-element.21), channel_id=1, source_target_pairs={{0,48},{16,0},{32,16},{48,32},{1,49},{17,1},{33,17},{49,33},{2,50}... | collective-permute-start | bytes 589832 | tf_op jit(solution)/shard_map/ppermute | solution.py:288
  146.0 17.2 %copy-start = (bf16[96,96]{1,0:T(8,128)(2,1)S(1)}, bf16[96,96]{1,0:T(8,128)(2,1)}, u32[]{:S(2)}) copy-start(bf16[96,96]{1,0:T(8,128)(2,1)} %constant.23.clone.table_ref) | copy-start | bytes 55300
